TPU v7x, 128 devices: a whole 4x4x4 slice. The times are simulated.
128 devices in a mesh: dp: 2 (over core), ep: 64 (over x, y, z).
Axes of the slice: x: 4, y: 4, z: 4, core: 2. Of those that a mesh axis runs over, the one named last changes fastest.
Arguments:
- x: bfloat16 [2, 64, 256, 2048], P('dp', 'ep'), parts along dimension 0
- expert: int32 [2, 64, 256, 6], P('dp', 'ep'), parts along dimension 0
- slot: int32 [2, 64, 256, 6], P('dp', 'ep'), parts along dimension 0
- gate: float32 [2, 64, 256, 6], P('dp', 'ep'), parts along dimension 0
- w_gate: bfloat16 [64, 2048, 1408], P('ep')
- w_up: bfloat16 [64, 2048, 1408], P('ep')
- w_down: bfloat16 [64, 1408, 2048], P('ep')
- s_gate: bfloat16 [2048, 2816], replicated
- s_up: bfloat16 [2048, 2816], replicated
- s_down: bfloat16 [2816, 2048], replicated
Outputs:
- y: bfloat16 [2, 64, 256, 2048], P('dp', 'ep'), parts along dimension 0
There are 2 independent parts. A program takes and returns all parts, laid end to end along the dimension named above; an argument that names none is the same for every part.
All inputs are finite; a program needn't handle non-finite values.
Results may differ from a plain program's by a relative error of at most 0.009.
Values are sent between devices in bfloat16 or wider.
A program may use at most 1.5 GiB of HBM per device.

v0:
```python
import jax
import jax.numpy as jnp
from jax import lax
from jax.sharding import NamedSharding, PartitionSpec as P


def einsum(form, a, b):
    return jnp.einsum(form, a.astype(jnp.float32), b.astype(jnp.float32))


def for_all(x, s_gate, s_up, s_down):
    h = jax.nn.silu(einsum("...d,df->...f", x, s_gate)) * einsum("...d,df->...f", x, s_up)
    return einsum("...f,fd->...d", h.astype(jnp.bfloat16), s_down)


def solution(mesh):
    def placed(v, *spec):
        return lax.with_sharding_constraint(v, NamedSharding(mesh, P(*spec)))

    def step(x, expert, slot, gate, w_gate, w_up, w_down, s_gate, s_up, s_down):
        experts, (tokens, top) = w_gate.shape[0], expert.shape[2:]
        slots = 5 * tokens * top // (4 * experts)
        to_expert = jax.nn.one_hot(expert, experts, dtype=jnp.bfloat16)
        to_slot = jax.nn.one_hot(slot, slots, dtype=jnp.bfloat16)
        weighted = to_expert * gate[..., None].astype(jnp.bfloat16)
        dispatch = einsum("abtke,abtkc->abtec", to_expert, to_slot).astype(jnp.bfloat16)
        combine = einsum("abtke,abtkc->abtec", weighted, to_slot).astype(jnp.bfloat16)
        z = einsum("abtec,abtd->aebcd", dispatch, x).astype(jnp.bfloat16)
        z = placed(z, "dp", None, "ep", None, None)
        z = placed(z, "dp", "ep", None, None, None)
        h = jax.nn.silu(einsum("aebcd,edf->aebcf", z, w_gate))
        h = (h * einsum("aebcd,edf->aebcf", z, w_up)).astype(jnp.bfloat16)
        out = einsum("aebcf,efd->aebcd", h, w_down).astype(jnp.bfloat16)
        out = placed(out, "dp", "ep", None, None, None)
        out = placed(out, "dp", None, "ep", None, None)
        y = einsum("abtec,aebcd->abtd", combine, out)
        return (y + for_all(x, s_gate, s_up, s_down)).astype(jnp.bfloat16)

    return step
```

profile of v0, /device:TPU:34, one launch (start us, length us, event | category | flops | bytes accessed | tf_op | source)
XLA Modules:
  0.0 373.4 jit_solution(14491118744415178748)
XLA Ops:
  0.0 0.0 copy-start
  0.0 0.9 copy.12
  0.9 0.8 copy.14
  1.7 3.5 fusion.41
  5.2 3.3 copy.11
  8.5 0.0 copy-done
  8.5 5.3 %convert_bitcast_fusion.1 = bf16[1,64,1,1,30,2048]{5,1,4,3,2,0:T(8,128)(2,1)} fusion(bf16[1,1,256,2048]{3,2,1,0:T(8,128)(2,1)S(1)} %copy-done, bf16[256,64,30]{0,1,2:T(8,128)(2,1)S(1)} %copy.11), kind=kOutput, calls=%fused_computation.14 | convolution fusion | flops 2017198080 | bytes 9895936 | tf_op jit(solution)/abtec,abtd->aebcd/dot_general | solution.py:8
  13.8 0.0 slice-start
  13.8 10.9 %copy.6 = bf16[1,64,1,1,30,2048]{5,4,3,2,0,1:T(8,128)(2,1)} copy(bf16[1,64,1,1,30,2048]{5,1,4,3,2,0:T(8,128)(2,1)} %convert_bitcast_fusion.1) | data formatting | bytes 15728640 | tf_op jit(solution)/sharding_constraint;jit(solution)/sharding_constraint | solution.py:18
  24.7 0.0 slice-start.1
  24.7 118.3 %all-to-all.4 = bf16[1,64,1,1,30,2048]{5,4,3,2,0,1:T(8,128)(2,1)S(1)} all-to-all(bf16[1,64,1,1,30,2048]{5,4,3,2,0,1:T(8,128)(2,1)} %copy.6), channel_id=1, replica_groups=mesh['dp'=2,'ep'=64] {'ep'}, dimensions={1} | all-to-all | bytes 15728640 | tf_op jit(solution)/sharding_constraint;jit(solution)/sharding_constraint | solution.py:18
  143.1 0.0 copy-start.1
  143.1 3.3 copy-done.1
  146.4 0.0 slice-done
  146.4 0.0 slice-done.1
  146.4 15.7 %fusion.6 = f32[64,30,1408]{2,0,1:T(8,128)} fusion(bf16[1,64,1,1,30,2048]{5,4,3,2,0,1:T(8,128)(2,1)S(1)} %all-to-all.4, bf16[1,2048,1408]{2,1,0:T(8,128)(2,1)S(1)} %bitcast.133), kind=kOutput, calls=%fused_computation.9 | convolution fusion | flops 11072962560 | bytes 24444928 | tf_op jit(solution)/aebcd,edf->aebcf/dot_general | solution.py:8
  162.0 39.8 %convert_bitcast_fusion = bf16[1,1,64,1,30,2048]{5,2,4,3,1,0:T(8,128)(2,1)} fusion(bf16[1,1408,2048]{2,1,0:T(8,128)(2,1)} %param.6, f32[64,30,1408]{2,0,1:T(8,128)} %fusion.6, bf16[1,64,1,1,30,2048]{5,4,3,2,0,1:T(8,128)(2,1)} %copy-done.1, bf16[1,2048,1408]{2,1,0:T(8,128)(2,1)} %param.4), kind=kOutput, calls=%fused_computation.13 | convolution fusion | flops 22166077440 | bytes 38076416 | tf_op jit(solution)/aebcf,efd->aebcd/dot_general | solution.py:8
  201.9 10.8 %copy.8 = bf16[1,1,64,1,30,2048]{5,4,3,1,0,2:T(8,128)(2,1)} copy(bf16[1,1,64,1,30,2048]{5,2,4,3,1,0:T(8,128)(2,1)} %convert_bitcast_fusion) | data formatting | bytes 15728640 | tf_op jit(solution)/sharding_constraint;jit(solution)/sharding_constraint | solution.py:18
  212.7 0.0 copy-start.3
  212.7 18.4 %all-to-all-start.1 = ((bf16[1,1,64,1,30,2048]{5,4,3,1,0,2:T(8,128)(2,1)}), bf16[1,1,64,1,30,2048]{5,4,3,1,0,2:T(8,128)(2,1)}, u32[]{:S(2)}, u32[]{:S(2)}) async-start(bf16[1,1,64,1,30,2048]{5,4,3,1,0,2:T(8,128)(2,1)} %copy.8), calls=%async_computation.1 | async-start | bytes 16777216 | tf_op jit(solution)/sharding_constraint;jit(solution)/sharding_constraint | solution.py:18
  231.1 0.0 copy-done.3
  231.1 0.1 copy.13
  231.3 3.0 fusion.45
  234.3 3.0 copy.10
  237.3 9.0 %convolution_bitcast_fusion.1 = f32[1,1,256,2816]{3,2,1,0:T(8,128)} fusion(bf16[2048,2816]{1,0:T(8,128)(2,1)} %param.7, bf16[1,1,256,2048]{3,2,1,0:T(8,128)(2,1)S(1)} %copy-done), kind=kOutput, calls=%fused_computation.24 | convolution fusion | flops 2952790016 | bytes 15466496 | tf_op jit(solution)/...d,df->...f/dot_general | solution.py:8
  246.3 0.0 copy-start.2
  246.3 16.0 %fusion.50 = f32[256,2048]{1,0:T(8,128)} fusion(bf16[2816,2048]{1,0:T(8,128)(2,1)} %param.9, bf16[2048,2816]{1,0:T(8,128)(2,1)} %param.8, f32[1,1,256,2816]{3,2,1,0:T(8,128)} %convolution_bitcast_fusion.1, bf16[1,1,256,2048]{3,2,1,0:T(8,128)(2,1)S(1)} %copy-done), kind=kOutput, calls=%fused_computation.43 | convolution fusion | flops 5909905408 | bytes 29097984 | tf_op jit(solution)/...f,fd->...d/dot_general | solution.py:8
  262.3 96.6 %all-to-all-done.1 = bf16[1,1,64,1,30,2048]{5,4,3,1,0,2:T(8,128)(2,1)} async-done(((bf16[1,1,64,1,30,2048]{5,4,3,1,0,2:T(8,128)(2,1)}), bf16[1,1,64,1,30,2048]{5,4,3,1,0,2:T(8,128)(2,1)}, u32[]{:S(2)}, u32[]{:S(2)}) %all-to-all-start.1) | async-done | bytes 7864352 | tf_op jit(solution)/sharding_constraint;jit(solution)/sharding_constraint | solution.py:18
  358.9 0.0 copy-done.2
  358.9 14.3 %fusion.33 = bf16[1,1,256,2048]{3,2,1,0:T(8,128)(2,1)} fusion(f32[256,2048]{1,0:T(8,128)} %fusion.50, bf16[1,1,64,1,30,2048]{5,4,3,1,0,2:T(8,128)(2,1)} %all-to-all-done.1, bf16[256,64,30]{0,1,2:T(8,128)(2,1)S(1)} %copy-done.2), kind=kOutput, calls=%fused_computation.30 | convolution fusion | flops 2014314496 | bytes 11993088 | tf_op jit(solution)/abtec,aebcd->abtd/dot_general | solution.py:8
  (2 shorter events, 0.0 us)
Async XLA Ops:
  0.0 8.5 %copy-start = (bf16[1,1,256,2048]{3,2,1,0:T(8,128)(2,1)S(1)}, bf16[1,1,256,2048]{3,2,1,0:T(8,128)(2,1)}, u32[]{:S(2)}) copy-start(bf16[1,1,256,2048]{3,2,1,0:T(8,128)(2,1)} %param.3) | copy-start | bytes 3145732
  13.8 132.6 %slice-start = ((s8[5767168]{0:T(1024)(128)(4,1)}), s8[1572864]{0:T(1024)(128)(4,1)S(1)}, s32[]{:S(2)}) async-start(s8[5767168]{0:T(1024)(128)(4,1)} %bitcast.132), calls=%async_computation.2 | async-start | bytes 3145728
  24.7 121.6 %slice-start.1 = ((s8[5767168]{0:T(1024)(128)(4,1)}), s8[4194304]{0:T(1024)(128)(4,1)S(1)}, s32[]{:S(2)}) async-start(s8[5767168]{0:T(1024)(128)(4,1)} %bitcast.132), calls=%async_computation.3 | async-start | bytes 8388608
  143.1 3.3 copy-start.1
  212.7 18.4 %copy-start.3 = (f32[1,1,256,6]{2,1,3,0:T(1,128)S(1)}, f32[1,1,256,6]{2,1,3,0:T(1,128)}, u32[]{:S(2)}) copy-start(f32[1,1,256,6]{2,1,3,0:T(1,128)} %param.1) | copy-start | bytes 18436
  212.7 146.2 %all-to-all-start.1 = ((bf16[1,1,64,1,30,2048]{5,4,3,1,0,2:T(8,128)(2,1)}), bf16[1,1,64,1,30,2048]{5,4,3,1,0,2:T(8,128)(2,1)}, u32[]{:S(2)}, u32[]{:S(2)}) async-start(bf16[1,1,64,1,30,2048]{5,4,3,1,0,2:T(8,128)(2,1)} %copy.8), calls=%async_computation.1 | async-start | bytes 16777216 | tf_op jit(solution)/sharding_constraint;jit(solution)/sharding_constraint | solution.py:18
  246.3 112.6 %copy-start.2 = (bf16[256,64,30]{0,1,2:T(8,128)(2,1)S(1)}, bf16[256,64,30]{0,1,2:T(8,128)(2,1)}, u32[]{:S(2)}) copy-start(bf16[256,64,30]{0,1,2:T(8,128)(2,1)} %copy.10) | copy-start | bytes 2949124
where the time goes:
time: 393 us; the launch traced here: 373 us
  blocking collectives  118 us (30%)
  waiting for transfers between devices  111 us (28%)
  matrix products  106 us (27%)
  local copies, waits for them, and re-layouts  33.4 us (8%)
  starting transfers between devices  15.8 us (4%)
    another operation x1, blocking collectives, placed(): return lax.with_sharding_constraint(v, NamedSharding(mesh, P(*spec)))  118 us
    another operation x1, waiting for transfers between devices, placed(): return lax.with_sharding_constraint(v, NamedSharding(mesh, P(*spec)))  111 us
    dot_general x8, matrix products, einsum(): return jnp.einsum(form, a.astype(jnp.float32), b.astype(jnp.float32))  106 us
    another operation x2, local copies, waits for them, and re-layouts, placed(): return lax.with_sharding_constraint(v, NamedSharding(mesh, P(*spec)))  21.8 us
    another operation x1, starting transfers between devices, placed(): return lax.with_sharding_constraint(v, NamedSharding(mesh, P(*spec)))  15.8 us
  transfers between devices with their start and end apart: 1, of which 1 were waited for; matrix products, arithmetic and copies ran while one was open for 8% of the time, Pallas kernels for 0%

commit v1 on v0

v1 whole, which is shorter than its diff:
```python
import functools

import jax
import jax.numpy as jnp
from jax import lax
from jax.experimental import pallas as pl
from jax.experimental.pallas import tpu as pltpu
from jax.sharding import PartitionSpec as P

MESH = pl.DeviceIdType.MESH
BF16, F32 = jnp.bfloat16, jnp.float32
S = 16
HALVES = 2
SPAN = S * HALVES
ALL = slice(None)


def silu_mul(g, u):
    return (jax.nn.silu(g) * u).astype(BF16)


def kernel(R, parts, shared_tile, top, names, *refs):
    (x_ref, m_ref, wg_hbm, wu_hbm, wd_hbm, sg_hbm, su_hbm, sd_hbm, y_ref) = refs[:9]
    xa, g_buf, h_buf, z_buf, ps = refs[9:12], refs[12:15], refs[15:18], refs[18:21], refs[21:24]
    (meta, wg, wu, wd, zcat, hb, yacc, sgb, sub, sdb,
     w_sem, sh_sem, m_s, m_r, a_s, a_r, b_s, b_r, c_s, c_r, c2_s, c2_r, b2_s, b2_r, a2_s, a2_r, h_free, g_free) = refs[24:]
    dp_axis, ep_axis = names
    T = x_ref.shape[0]
    FF = wg.shape[1]
    KR = R * R * S
    dp, me = lax.axis_index(dp_axis), lax.axis_index(ep_axis)
    pos = (me // (R * R), lax.rem(me // R, R), lax.rem(me, R))
    unit = (R * R, R, 1)
    edges = [0]
    for c in parts:
        edges.append(edges[-1] + c)
    cols = [slice(edges[k], edges[k + 1]) for k in range(3)]

    def peer(axis, r):
        return me + (lax.rem(pos[axis] + r, R) - pos[axis]) * unit[axis]

    def zsl(k, a, b, c):
        i = [None] * 3
        i[k], i[(k + 1) % 3], i[(k + 2) % 3] = a, b, c
        return tuple(i)

    def hsl(k, a, b):
        return (a, b) if k < 2 else (b, a)

    def send(src, dst, s, r, axis, step):
        pltpu.make_async_remote_copy(
            src_ref=src, dst_ref=dst, send_sem=s, recv_sem=r,
            device_id=(dp, peer(axis, step)), device_id_type=MESH,
        ).start()

    def pend(ref, s, r):
        return pltpu.make_async_remote_copy(
            src_ref=ref, dst_ref=ref, send_sem=s, recv_sem=r,
            device_id=(dp, peer(0, 1)), device_id_type=MESH,
        )

    def whole(k, h):
        return g_buf[k].at[h, 1:R]

    n_sh = sg_hbm.shape[1] // shared_tile

    def sh_copies(j, slot):
        at = pl.ds(pl.multiple_of(j * shared_tile, shared_tile), shared_tile)
        return (
            pltpu.make_async_copy(sg_hbm.at[:, at], sgb.at[slot], sh_sem.at[slot, 0]),
            pltpu.make_async_copy(su_hbm.at[:, at], sub.at[slot], sh_sem.at[slot, 1]),
            pltpu.make_async_copy(sd_hbm.at[at], sdb.at[slot], sh_sem.at[slot, 2]),
        )

    for c in sh_copies(0, 0):
        c.start()

    barrier = pltpu.get_barrier_semaphore()
    for axis in range(3):
        for r in range(1, R):
            pl.semaphore_signal(barrier, inc=1, device_id=(dp, peer(axis, r)), device_id_type=MESH)
    pl.semaphore_wait(barrier, 3 * (R - 1))

    for k in range(3):
        for r in range(1, R):
            send(m_ref, meta.at[k, R - r], m_s.at[k], m_r.at[k], k, r)
    for r in range(1, R):
        for k in range(3):
            send(x_ref.at[:, cols[k]], xa[k].at[R - r], a_s.at[k], a_r.at[k], k, r)
    for k in range(3):
        meta[k, 0] = m_ref[...]
        xa[k][0] = x_ref[:, cols[k]]

    yacc[...] = jnp.zeros_like(yacc)

    @pl.loop(0, n_sh)
    def _(j):
        slot = lax.rem(j, 2)
        for c in sh_copies(j, slot):
            c.wait()

        @pl.when(j + 1 < n_sh)
        def _():
            for c in sh_copies(j + 1, 1 - slot):
                c.start()

        g = jnp.dot(x_ref[...], sgb[slot], preferred_element_type=F32)
        u = jnp.dot(x_ref[...], sub[slot], preferred_element_type=F32)
        yacc[...] += jnp.dot(silu_mul(g, u), sdb[slot], preferred_element_type=F32)

    w_copies = [
        pltpu.make_async_copy(src, dst, w_sem.at[i])
        for i, (src, dst) in enumerate(((wg_hbm, wg), (wu_hbm, wu), (wd_hbm, wd)))
    ]
    for c in w_copies:
        c.start()

    def slot_ids(k, h):
        row = lax.broadcasted_iota(jnp.int32, (KR, T), 0)
        rb, rc, s = row // (R * S), lax.rem(row // S, R), lax.rem(row, S)
        b, c = (k + 1) % 3, (k + 2) % 3
        e = pos[k] * unit[k] + lax.rem(rb + pos[b], R) * unit[b] + lax.rem(rc + pos[c], R) * unit[c]
        return (e * SPAN + s + h * S).astype(F32)

    def gather(k, h):
        ids = slot_ids(k, h)

        @pl.loop(0, R)
        def _(ra):
            hit = ids == meta[k, ra, 0:1, :]
            for j in range(1, top):
                hit = hit | (ids == meta[k, ra, j:j + 1, :])
            pick = jnp.where(hit, 1.0, 0.0).astype(BF16)
            rows = jnp.dot(pick, xa[k][ra], preferred_element_type=F32).astype(BF16)
            rows = rows.reshape(R, R, S, parts[k])
            g_buf[k][h, 1:R, :, ra] = rows[1:]
            z_buf[k][(h,) + zsl(k, ra, 0, 0)] = rows[0, 0]
            h_buf[k][(h, ALL) + hsl(k, ra, 0)] = rows[0, 1:]

    def send_b(k, h):
        for rb in range(1, R):
            to = R - rb
            send(g_buf[k].at[h, rb, 1:R], h_buf[k].at[(h, ALL) + hsl(k, ALL, to)],
                 b_s.at[k, h], b_r.at[k, h], (k + 1) % 3, rb)
            send(g_buf[k].at[h, rb, 0], z_buf[k].at[(h,) + zsl(k, ALL, to, 0)],
                 b_s.at[k, h], b_r.at[k, h], (k + 1) % 3, rb)

    def relay_c(h):
        for k in range(3):
            pend(whole(k, h), b_s.at[k, h], b_r.at[k, h]).wait_recv()
            for rc in range(1, R):
                send(h_buf[k].at[h, rc - 1], z_buf[k].at[(h,) + zsl(k, ALL, ALL, R - rc)],
                     c_s.at[k, h], c_r.at[k, h], (k + 2) % 3, rc)

    for k in range(3):
        pend(meta.at[k, 1:R], m_s.at[k], m_r.at[k]).wait_recv()
        pend(xa[k].at[1:R], a_s.at[k], a_r.at[k]).wait_recv()
        gather(k, 0)
        send_b(k, 0)
    for k in range(3):
        gather(k, 1)
    relay_c(0)
    for k in range(3):
        send_b(k, 1)

    for c in w_copies:
        c.wait()

    def send_c2(h, rx):
        for k in range(3):
            s, r, axis = c2_s.at[k, h], c2_r.at[k, h], (k + 2) % 3
            z, hh, g = z_buf[k], h_buf[k], g_buf[k]
            if k == 0:
                for rc in range(1, R):
                    send(z.at[h, rx, 1:R, rc], hh.at[h, R - rc - 1, rx, 1:R], s, r, axis, rc)
                    send(z.at[h, rx, 0, rc], g.at[h, 0, R - rc, rx], s, r, axis, rc)
            elif k == 1:
                @pl.when(rx > 0)
                def _():
                    send(z.at[h, rx, :, 1:R], hh.at[h, R - rx - 1, :, 1:R], s, r, axis, rx)
                    send(z.at[h, rx, :, 0], g.at[h, 0, R - rx], s, r, axis, rx)
            else:
                @pl.when(rx > 0)
                def _():
                    for rc in range(1, R):
                        send(z.at[h, rx, rc], hh.at[h, R - rc - 1, rx], s, r, axis, rc)

                @pl.when(rx == 0)
                def _():
                    for rc in range(1, R):
                        send(z.at[h, rx, rc], g.at[h, 0, R - rc], s, r, axis, rc)

    def relay_b2(h):
        for k in range(3):
            pend(whole(k, h), c2_s.at[k, h], c2_r.at[k, h]).wait_recv()
            pl.semaphore_wait(g_free.at[k, h], R - 1)
            for rb in range(1, R):
                s, r, axis, to = b2_s.at[k, h], b2_r.at[k, h], (k + 1) % 3, R - rb
                send(h_buf[k].at[(h, ALL) + hsl(k, ALL, rb)], g_buf[k].at[h, to, 1:R], s, r, axis, rb)
                send(z_buf[k].at[(h,) + zsl(k, ALL, rb, 0)], g_buf[k].at[h, to, 0], s, r, axis, rb)

    wide = [(n, min(512, FF - n)) for n in range(0, FF, 512)]

    @pl.loop(0, HALVES * R)
    def _(t):
        h, rx = t // R, lax.rem(t, R)

        @pl.when(rx == 0)
        def _():
            for k in range(3):
                pend(whole(k, h), c_s.at[k, h], c_r.at[k, h]).wait_recv()
            for k in range(3):
                pend(whole(k, h), c_s.at[k, h], c_r.at[k, h]).wait_send()
                pend(whole(k, h), b_s.at[k, h], b_r.at[k, h]).wait_send()
                for free, axis in ((h_free, k + 2), (g_free, k + 1)):
                    for r in range(1, R):
                        pl.semaphore_signal(free.at[k, h], inc=1, device_id=(dp, peer(axis % 3, r)), device_id_type=MESH)

        for k in range(3):
            zcat[:, cols[k]] = z_buf[k][h, rx].reshape(KR, parts[k])
        for n, w in wide:
            g = jnp.dot(zcat[...], wg[:, n:n + w], preferred_element_type=F32)
            u = jnp.dot(zcat[...], wu[:, n:n + w], preferred_element_type=F32)
            hb[:, n:n + w] = silu_mul(g, u)
        for k in range(3):
            o = jnp.dot(hb[...], wd[:, cols[k]], preferred_element_type=F32)
            z_buf[k][h, rx] = o.astype(BF16).reshape(R, R, S, parts[k])

        @pl.when(rx == 0)
        def _():
            for k in range(3):
                pl.semaphore_wait(h_free.at[k, h], R - 1)

        send_c2(h, rx)

        @pl.when(t == R // 2 - 1)
        def _():
            relay_c(1)

        @pl.when(t == R + R // 2 - 1)
        def _():
            relay_b2(0)

    def own_rows(k, h):
        g_buf[k][h, 0, 0] = z_buf[k][(h,) + zsl(k, ALL, 0, 0)]

    def weighted(k, ra, h):
        ids = slot_ids(k, h)
        w = jnp.zeros((KR, T), F32)
        for j in range(top):
            w += jnp.where(ids == meta[k, ra, j:j + 1, :], meta[k, ra, 8 + j:9 + j, :], 0.0)
        rows = g_buf[k][h, :, :, ra].reshape(KR, parts[k])
        return lax.dot_general(w.astype(BF16), rows, (((0,), (0,)), ((), ())), preferred_element_type=F32)

    for k in range(3):
        for h in range(HALVES):
            own_rows(k, h)
    for k in range(3):
        pend(whole(k, 0), b2_s.at[k, 0], b2_r.at[k, 0]).wait_recv()
        yacc[:, cols[k]] += weighted(k, 0, 0)
    relay_b2(1)
    for k in range(3):
        pend(whole(k, 1), b2_s.at[k, 1], b2_r.at[k, 1]).wait_recv()

        @pl.loop(1, R)
        def _(ra):
            ps[k][ra - 1] = (weighted(k, ra, 0) + weighted(k, ra, 1)).astype(BF16)
            send(ps[k].at[ra - 1], xa[k].at[R - ra], a2_s.at[k], a2_r.at[k], k, ra)

    for k in range(3):
        yacc[:, cols[k]] += weighted(k, 0, 1)
    for k in range(3):
        pend(xa[k].at[1:R], a2_s.at[k], a2_r.at[k]).wait_recv()
        total = yacc[:, cols[k]]
        for ra in range(1, R):
            total += xa[k][ra].astype(F32)
        y_ref[:, cols[k]] = total.astype(BF16)

    for k in range(3):
        pend(meta.at[k, 1:R], m_s.at[k], m_r.at[k]).wait_send()
        pend(xa[k].at[1:R], a_s.at[k], a_r.at[k]).wait_send()
        pend(xa[k].at[1:R], a2_s.at[k], a2_r.at[k]).wait_send()
        for h in range(HALVES):
            for s, r in ((c2_s, c2_r), (b2_s, b2_r)):
                pend(whole(k, h), s.at[k, h], r.at[k, h]).wait_send()


def split(d):
    tiles = d // 128
    low = tiles // 3
    sizes = [low, low, low]
    for i in range(tiles - 3 * low):
        sizes[2 - i] += 1
    return [128 * n for n in sizes]


def solution(mesh):
    names = ("dp", "ep")

    def step(x, expert, slot, gate, w_gate, w_up, w_down, s_gate, s_up, s_down):
        R = round(mesh.shape["ep"] ** (1 / 3))
        T, D = x.shape[2:]
        top, members = expert.shape[-1], mesh.shape["ep"]
        FF, SFF = w_gate.shape[-1], s_gate.shape[-1]
        slots = 5 * T * top // (4 * members)
        parts = split(D)
        x, expert, slot, gate = x[0, 0], expert[0, 0], slot[0, 0], gate[0, 0]
        key = jnp.where(slot < slots, expert * SPAN + slot, -1).astype(F32)
        weight = gate.astype(BF16).astype(F32)
        m = jnp.concatenate([jnp.pad(key.T, ((0, 8 - top), (0, 0))), jnp.pad(weight.T, ((0, 8 - top), (0, 0)))], 0)
        any_space = pl.BlockSpec(memory_space=pl.ANY)
        vmem = pl.BlockSpec(memory_space=pltpu.VMEM)
        tile = min(256, SFF)
        dma = pltpu.SemaphoreType.DMA
        scratch = (
            [pltpu.VMEM((R, T, c), BF16) for c in parts]
            + [pltpu.VMEM((HALVES, R, R, R, S, c), BF16) for c in parts]
            + [pltpu.VMEM((HALVES, R - 1, R, R, S, c), BF16) for c in parts]
            + [pltpu.VMEM((HALVES, R, R, R, S, c), BF16) for c in parts]
            + [pltpu.VMEM((R - 1, T, c), BF16) for c in parts]
            + [pltpu.VMEM((3, R, 16, T), F32)]
            + [pltpu.VMEM((D, FF), BF16), pltpu.VMEM((D, FF), BF16), pltpu.VMEM((FF, D), BF16)]
            + [pltpu.VMEM((R * R * S, D), BF16), pltpu.VMEM((R * R * S, FF), BF16), pltpu.VMEM((T, D), F32)]
            + [pltpu.VMEM((2, D, tile), BF16), pltpu.VMEM((2, D, tile), BF16), pltpu.VMEM((2, tile, D), BF16)]
            + [dma((3,)), dma((2, 3))]
            + [dma((3,))] * 4 + [dma((3, HALVES))] * 8 + [dma((3,))] * 2
            + [pltpu.SemaphoreType.REGULAR((3, HALVES))] * 2
        )
        y = pl.pallas_call(
            functools.partial(kernel, R, parts, tile, top, names),
            out_shape=jax.ShapeDtypeStruct((T, D), BF16),
            in_specs=[vmem, vmem] + [any_space] * 6,
            out_specs=vmem,
            scratch_shapes=scratch,
            compiler_params=pltpu.CompilerParams(
                collective_id=0, has_side_effects=True, vmem_limit_bytes=67043328
            ),
            name="moe",
        )(x, m, w_gate[0], w_up[0], w_down[0], s_gate, s_up, s_down)
        return y[None, None]

    tok = P("dp", "ep", None, None)
    exp = P("ep", None, None)
    rep = P(None, None)
    return jax.shard_map(
        step, mesh=mesh,
        in_specs=(tok, tok, tok, tok, exp, exp, exp, rep, rep, rep),
        out_specs=tok, check_vma=False,
    )
```

time: 393 us -> 201 us (0.51)
  the two profiles are of different devices: /device:TPU:34 before, /device:TPU:30 now
where the time goes in v1:
time: 201 us; the launch traced here: 200 us
  Pallas kernels  196 us (98%)
  local copies, waits for them, and re-layouts  3 us (1%)
    pallas_call x1, Pallas kernels, step(): pl.pallas_call(functools.partial(kernel, R, parts, tile, top, names), out...  196 us

profile of v1, /device:TPU:30, one launch (start us, length us, event | category | flops | bytes accessed | tf_op | source)
XLA Modules:
  0.0 200.5 jit_solution(16711410573775534802)
XLA Ops:
  0.0 0.7 copy.31
  0.7 0.7 fusion.2
  1.4 0.6 select_maximum_fusion.refs_1_
  2.0 196.1 %moe.1 = bf16[256,2048]{1,0:T(8,128)(2,1)} custom-call(bf16[256,2048]{1,0:T(8,128)(2,1)} %bitcast.18, f32[16,256]{1,0:T(8,128)} %select_maximum_fusion.refs_1_, bf16[2048,1408]{1,0:T(8,128)(2,1)} %bitcast.14, bf16[2048,1408]{1,0:T(8,128)(2,1)} %bitcast.15, bf16[1408,2048]{1,0:T(8,128)(2,1)} %bitcast.16, bf16[2048,2816]{1,0:T(8,128)(2,1)} %refs_5_.1, ...), custom_call_target="tpu_custom_call" | custom-call | tf_op jit(solution)/shard_map/moe/pallas_call | solution.py:329
  198.2 2.3 %copy.33 = bf16[1,1,256,2048]{3,2,1,0:T(8,128)(2,1)} copy(bf16[1,1,256,2048]{3,2,1,0:T(8,128)(2,1)} %bitcast.17) | data formatting | bytes 2097152
  (1 shorter events, 0.0 us)

commit v2 on v1

--- a/solution.py
+++ b/solution.py
@@ -36,6 +36,9 @@
         edges.append(edges[-1] + c)
     cols = [slice(edges[k], edges[k + 1]) for k in range(3)]
 
+    order = sorted(range(3), key=lambda k: -parts[k])
+    near = sorted(range(1, R), key=lambda r: (min(r, R - r), -r))
+
     def peer(axis, r):
         return me + (lax.rem(pos[axis] + r, R) - pos[axis]) * unit[axis]
 
@@ -75,38 +78,83 @@
     for c in sh_copies(0, 0):
         c.start()
 
+    def shared(j):
+        slot = lax.rem(j, 2)
+        for c in sh_copies(j, slot):
+            c.wait()
+
+        @pl.when(j + 1 < n_sh)
+        def _():
+            for c in sh_copies(j + 1, 1 - slot):
+                c.start()
+
+        g = jnp.dot(x_ref[...], sgb[slot], preferred_element_type=F32)
+        u = jnp.dot(x_ref[...], sub[slot], preferred_element_type=F32)
+        yacc[...] += jnp.dot(silu_mul(g, u), sdb[slot], preferred_element_type=F32)
+
+    def slot_ids(k, h):
+        row = lax.broadcasted_iota(jnp.int32, (KR, T), 0)
+        rb, rc, s = row // (R * S), lax.rem(row // S, R), lax.rem(row, S)
+        b, c = (k + 1) % 3, (k + 2) % 3
+        e = pos[k] * unit[k] + lax.rem(rb + pos[b], R) * unit[b] + lax.rem(rc + pos[c], R) * unit[c]
+        return (e * SPAN + s + h * S).astype(F32)
+
+    def gather(k, h, ra, ids):
+        hit = ids == meta[k, ra, 0:1, :]
+        for j in range(1, top):
+            hit = hit | (ids == meta[k, ra, j:j + 1, :])
+        pick = jnp.where(hit, 1.0, 0.0).astype(BF16)
+        rows = jnp.dot(pick, xa[k][ra], preferred_element_type=F32).astype(BF16)
+        rows = rows.reshape(R, R, S, parts[k])
+        g_buf[k][h, 1:R, :, ra] = rows[1:]
+        z_buf[k][(h,) + zsl(k, ra, 0, 0)] = rows[0, 0]
+        h_buf[k][(h, ALL) + hsl(k, ra, 0)] = rows[0, 1:]
+
+    def send_b(k, h, ra):
+        for rb in near:
+            to = R - rb
+            send(g_buf[k].at[h, rb, 1:R, ra], h_buf[k].at[(h, ALL) + hsl(k, ra, to)],
+                 b_s.at[k, h], b_r.at[k, h, ra], (k + 1) % 3, rb)
+            send(g_buf[k].at[h, rb, 0, ra], z_buf[k].at[(h,) + zsl(k, ra, to, 0)],
+                 b_s.at[k, h], b_r.at[k, h, ra], (k + 1) % 3, rb)
+
+    @jax.named_scope("relay_c")
+    def relay_c(h, ra):
+        for k in order:
+            pend(g_buf[k].at[h, 1:R, :, 0], b_s.at[k, h], b_r.at[k, h, ra]).wait_recv()
+            for rc in near:
+                send(h_buf[k].at[(h, rc - 1) + hsl(k, ra, ALL)], z_buf[k].at[(h,) + zsl(k, ra, ALL, R - rc)],
+                     c_s.at[k, h], c_r.at[k, h], (k + 2) % 3, rc)
+
     barrier = pltpu.get_barrier_semaphore()
     for axis in range(3):
         for r in range(1, R):
             pl.semaphore_signal(barrier, inc=1, device_id=(dp, peer(axis, r)), device_id_type=MESH)
-    pl.semaphore_wait(barrier, 3 * (R - 1))
-
-    for k in range(3):
-        for r in range(1, R):
-            send(m_ref, meta.at[k, R - r], m_s.at[k], m_r.at[k], k, r)
-    for r in range(1, R):
-        for k in range(3):
-            send(x_ref.at[:, cols[k]], xa[k].at[R - r], a_s.at[k], a_r.at[k], k, r)
+
     for k in range(3):
         meta[k, 0] = m_ref[...]
         xa[k][0] = x_ref[:, cols[k]]
-
     yacc[...] = jnp.zeros_like(yacc)
 
-    @pl.loop(0, n_sh)
-    def _(j):
-        slot = lax.rem(j, 2)
-        for c in sh_copies(j, slot):
-            c.wait()
-
-        @pl.when(j + 1 < n_sh)
-        def _():
-            for c in sh_copies(j + 1, 1 - slot):
-                c.start()
-
-        g = jnp.dot(x_ref[...], sgb[slot], preferred_element_type=F32)
-        u = jnp.dot(x_ref[...], sub[slot], preferred_element_type=F32)
-        yacc[...] += jnp.dot(silu_mul(g, u), sdb[slot], preferred_element_type=F32)
+    @pl.loop(0, HALVES)
+    @jax.named_scope("gather")
+    def _(h):
+        for k in order:
+            gather(k, h, 0, slot_ids(k, h))
+
+    with jax.named_scope("barrier"):
+        pl.semaphore_wait(barrier, 3 * (R - 1))
+
+    for k in order:
+        for r in near:
+            send(m_ref, meta.at[k, R - r], m_s.at[k], m_r.at[k], k, r)
+    for r in near:
+        for k in order:
+            send(x_ref.at[:, cols[k]], xa[k].at[R - r], a_s.at[k], a_r.at[k], k, r)
+    for k in order:
+        send_b(k, 0, 0)
+
+    pl.loop(0, n_sh - R)(jax.named_scope("shared")(shared))
 
     w_copies = [
         pltpu.make_async_copy(src, dst, w_sem.at[i])
@@ -115,89 +163,76 @@
     for c in w_copies:
         c.start()
 
-    def slot_ids(k, h):
-        row = lax.broadcasted_iota(jnp.int32, (KR, T), 0)
-        rb, rc, s = row // (R * S), lax.rem(row // S, R), lax.rem(row, S)
-        b, c = (k + 1) % 3, (k + 2) % 3
-        e = pos[k] * unit[k] + lax.rem(rb + pos[b], R) * unit[b] + lax.rem(rc + pos[c], R) * unit[c]
-        return (e * SPAN + s + h * S).astype(F32)
-
-    def gather(k, h):
-        ids = slot_ids(k, h)
-
-        @pl.loop(0, R)
+    for k in order:
+        with jax.named_scope("wait_a"):
+            pend(meta.at[k, 1:R], m_s.at[k], m_r.at[k]).wait_recv()
+            pend(xa[k].at[1:R], a_s.at[k], a_r.at[k]).wait_recv()
+        ids = slot_ids(k, 0)
+
+        @pl.loop(1, R)
+        @jax.named_scope("gather")
         def _(ra):
-            hit = ids == meta[k, ra, 0:1, :]
-            for j in range(1, top):
-                hit = hit | (ids == meta[k, ra, j:j + 1, :])
-            pick = jnp.where(hit, 1.0, 0.0).astype(BF16)
-            rows = jnp.dot(pick, xa[k][ra], preferred_element_type=F32).astype(BF16)
-            rows = rows.reshape(R, R, S, parts[k])
-            g_buf[k][h, 1:R, :, ra] = rows[1:]
-            z_buf[k][(h,) + zsl(k, ra, 0, 0)] = rows[0, 0]
-            h_buf[k][(h, ALL) + hsl(k, ra, 0)] = rows[0, 1:]
-
-    def send_b(k, h):
-        for rb in range(1, R):
-            to = R - rb
-            send(g_buf[k].at[h, rb, 1:R], h_buf[k].at[(h, ALL) + hsl(k, ALL, to)],
-                 b_s.at[k, h], b_r.at[k, h], (k + 1) % 3, rb)
-            send(g_buf[k].at[h, rb, 0], z_buf[k].at[(h,) + zsl(k, ALL, to, 0)],
-                 b_s.at[k, h], b_r.at[k, h], (k + 1) % 3, rb)
-
-    def relay_c(h):
-        for k in range(3):
-            pend(whole(k, h), b_s.at[k, h], b_r.at[k, h]).wait_recv()
-            for rc in range(1, R):
-                send(h_buf[k].at[h, rc - 1], z_buf[k].at[(h,) + zsl(k, ALL, ALL, R - rc)],
-                     c_s.at[k, h], c_r.at[k, h], (k + 2) % 3, rc)
-
-    for k in range(3):
-        pend(meta.at[k, 1:R], m_s.at[k], m_r.at[k]).wait_recv()
-        pend(xa[k].at[1:R], a_s.at[k], a_r.at[k]).wait_recv()
-        gather(k, 0)
-        send_b(k, 0)
-    for k in range(3):
-        gather(k, 1)
-    relay_c(0)
-    for k in range(3):
-        send_b(k, 1)
+            gather(k, 0, ra, ids)
+            send_b(k, 0, ra)
+
+    for k in order:
+        ids = slot_ids(k, 1)
+
+        @pl.loop(1, R)
+        @jax.named_scope("gather")
+        def _(ra):
+            gather(k, 1, ra, ids)
+
+    @pl.loop(0, R)
+    def _(ra):
+        with jax.named_scope("shared"):
+            shared(n_sh - R + ra)
+        relay_c(0, ra)
+        for k in order:
+            send_b(k, 1, ra)
 
     for c in w_copies:
         c.wait()
 
     def send_c2(h, rx):
-        for k in range(3):
-            s, r, axis = c2_s.at[k, h], c2_r.at[k, h], (k + 2) % 3
+        for k in order:
+            s, axis = c2_s.at[k, h], (k + 2) % 3
             z, hh, g = z_buf[k], h_buf[k], g_buf[k]
             if k == 0:
-                for rc in range(1, R):
-                    send(z.at[h, rx, 1:R, rc], hh.at[h, R - rc - 1, rx, 1:R], s, r, axis, rc)
-                    send(z.at[h, rx, 0, rc], g.at[h, 0, R - rc, rx], s, r, axis, rc)
+                for rc in near:
+                    send(z.at[h, rx, 1:R, rc], hh.at[h, R - rc - 1, rx, 1:R], s, c2_r.at[k, h, R - rc], axis, rc)
+                    send(z.at[h, rx, 0, rc], g.at[h, 0, R - rc, rx], s, c2_r.at[k, h, R - rc], axis, rc)
             elif k == 1:
                 @pl.when(rx > 0)
                 def _():
-                    send(z.at[h, rx, :, 1:R], hh.at[h, R - rx - 1, :, 1:R], s, r, axis, rx)
-                    send(z.at[h, rx, :, 0], g.at[h, 0, R - rx], s, r, axis, rx)
+                    send(z.at[h, rx, :, 1:R], hh.at[h, R - rx - 1, :, 1:R], s, c2_r.at[k, h, R - rx], axis, rx)
+                    send(z.at[h, rx, :, 0], g.at[h, 0, R - rx], s, c2_r.at[k, h, R - rx], axis, rx)
             else:
                 @pl.when(rx > 0)
                 def _():
-                    for rc in range(1, R):
-                        send(z.at[h, rx, rc], hh.at[h, R - rc - 1, rx], s, r, axis, rc)
+                    for rc in near:
+                        send(z.at[h, rx, rc], hh.at[h, R - rc - 1, rx], s, c2_r.at[k, h, R - rc], axis, rc)
 
                 @pl.when(rx == 0)
                 def _():
-                    for rc in range(1, R):
-                        send(z.at[h, rx, rc], g.at[h, 0, R - rc], s, r, axis, rc)
-
+                    for rc in near:
+                        send(z.at[h, rx, rc], g.at[h, 0, R - rc], s, c2_r.at[k, h, R - rc], axis, rc)
+
+    def own_b2(h):
+        for k in order:
+            pl.semaphore_wait(g_free.at[k, h], R - 1)
+            for rb in near:
+                send(z_buf[k].at[(h,) + zsl(k, ALL, rb, 0)], g_buf[k].at[h, R - rb, 0],
+                     b2_s.at[k, h], b2_r.at[k, h], (k + 1) % 3, rb)
+
+    @jax.named_scope("relay_b2")
     def relay_b2(h):
-        for k in range(3):
-            pend(whole(k, h), c2_s.at[k, h], c2_r.at[k, h]).wait_recv()
-            pl.semaphore_wait(g_free.at[k, h], R - 1)
-            for rb in range(1, R):
-                s, r, axis, to = b2_s.at[k, h], b2_r.at[k, h], (k + 1) % 3, R - rb
-                send(h_buf[k].at[(h, ALL) + hsl(k, ALL, rb)], g_buf[k].at[h, to, 1:R], s, r, axis, rb)
-                send(z_buf[k].at[(h,) + zsl(k, ALL, rb, 0)], g_buf[k].at[h, to, 0], s, r, axis, rb)
+        for ce in range(R - 1, 0, -1):
+            for k in order:
+                pend(g_buf[k].at[h, 1], c2_s.at[k, h], c2_r.at[k, h, ce]).wait_recv()
+                for rb in near:
+                    send(h_buf[k].at[(h, ce - 1) + hsl(k, ALL, rb)], g_buf[k].at[h, R - rb, ce],
+                         b2_s.at[k, h], b2_r.at[k, h], (k + 1) % 3, rb)
 
     wide = [(n, min(512, FF - n)) for n in range(0, FF, 512)]
 
@@ -206,6 +241,7 @@
         h, rx = t // R, lax.rem(t, R)
 
         @pl.when(rx == 0)
+        @jax.named_scope("wait_c")
         def _():
             for k in range(3):
                 pend(whole(k, h), c_s.at[k, h], c_r.at[k, h]).wait_recv()
@@ -216,15 +252,23 @@
                     for r in range(1, R):
                         pl.semaphore_signal(free.at[k, h], inc=1, device_id=(dp, peer(axis % 3, r)), device_id_type=MESH)
 
-        for k in range(3):
-            zcat[:, cols[k]] = z_buf[k][h, rx].reshape(KR, parts[k])
-        for n, w in wide:
-            g = jnp.dot(zcat[...], wg[:, n:n + w], preferred_element_type=F32)
-            u = jnp.dot(zcat[...], wu[:, n:n + w], preferred_element_type=F32)
-            hb[:, n:n + w] = silu_mul(g, u)
-        for k in range(3):
-            o = jnp.dot(hb[...], wd[:, cols[k]], preferred_element_type=F32)
-            z_buf[k][h, rx] = o.astype(BF16).reshape(R, R, S, parts[k])
+        @pl.when(t == 0)
+        def _():
+            @pl.loop(0, R // 2)
+            def _(ra):
+                relay_c(1, ra)
+
+        with jax.named_scope("up"):
+            for k in range(3):
+                zcat[:, cols[k]] = z_buf[k][h, rx].reshape(KR, parts[k])
+            for n, w in wide:
+                g = jnp.dot(zcat[...], wg[:, n:n + w], preferred_element_type=F32)
+                u = jnp.dot(zcat[...], wu[:, n:n + w], preferred_element_type=F32)
+                hb[:, n:n + w] = silu_mul(g, u)
+        with jax.named_scope("down"):
+            for k in range(3):
+                o = jnp.dot(hb[...], wd[:, cols[k]], preferred_element_type=F32)
+                z_buf[k][h, rx] = o.astype(BF16).reshape(R, R, S, parts[k])
 
         @pl.when(rx == 0)
         def _():
@@ -233,9 +277,15 @@
 
         send_c2(h, rx)
 
-        @pl.when(t == R // 2 - 1)
-        def _():
-            relay_c(1)
+        @pl.when(t == 0)
+        def _():
+            @pl.loop(R // 2, R)
+            def _(ra):
+                relay_c(1, ra)
+
+        @pl.when(rx == R - 1)
+        def _():
+            own_b2(h)
 
         @pl.when(t == R + R // 2 - 1)
         def _():
@@ -252,25 +302,31 @@
         rows = g_buf[k][h, :, :, ra].reshape(KR, parts[k])
         return lax.dot_general(w.astype(BF16), rows, (((0,), (0,)), ((), ())), preferred_element_type=F32)
 
-    for k in range(3):
+    relay_b2(1)
+    for k in order:
         for h in range(HALVES):
             own_rows(k, h)
-    for k in range(3):
-        pend(whole(k, 0), b2_s.at[k, 0], b2_r.at[k, 0]).wait_recv()
-        yacc[:, cols[k]] += weighted(k, 0, 0)
-    relay_b2(1)
-    for k in range(3):
-        pend(whole(k, 1), b2_s.at[k, 1], b2_r.at[k, 1]).wait_recv()
+    for k in order:
+        with jax.named_scope("wait_b2"):
+            pend(whole(k, 0), b2_s.at[k, 0], b2_r.at[k, 0]).wait_recv()
+        with jax.named_scope("weigh_own"):
+            yacc[:, cols[k]] += weighted(k, 0, 0)
+    for k in order:
+        with jax.named_scope("wait_b2"):
+            pend(whole(k, 1), b2_s.at[k, 1], b2_r.at[k, 1]).wait_recv()
 
         @pl.loop(1, R)
+        @jax.named_scope("weigh")
         def _(ra):
             ps[k][ra - 1] = (weighted(k, ra, 0) + weighted(k, ra, 1)).astype(BF16)
             send(ps[k].at[ra - 1], xa[k].at[R - ra], a2_s.at[k], a2_r.at[k], k, ra)
 
-    for k in range(3):
-        yacc[:, cols[k]] += weighted(k, 0, 1)
-    for k in range(3):
-        pend(xa[k].at[1:R], a2_s.at[k], a2_r.at[k]).wait_recv()
+    for k in order:
+        with jax.named_scope("weigh_own"):
+            yacc[:, cols[k]] += weighted(k, 0, 1)
+    for k in order:
+        with jax.named_scope("wait_a2"):
+            pend(xa[k].at[1:R], a2_s.at[k], a2_r.at[k]).wait_recv()
         total = yacc[:, cols[k]]
         for ra in range(1, R):
             total += xa[k][ra].astype(F32)
@@ -323,7 +379,9 @@
             + [pltpu.VMEM((R * R * S, D), BF16), pltpu.VMEM((R * R * S, FF), BF16), pltpu.VMEM((T, D), F32)]
             + [pltpu.VMEM((2, D, tile), BF16), pltpu.VMEM((2, D, tile), BF16), pltpu.VMEM((2, tile, D), BF16)]
             + [dma((3,)), dma((2, 3))]
-            + [dma((3,))] * 4 + [dma((3, HALVES))] * 8 + [dma((3,))] * 2
+            + [dma((3,))] * 4
+            + [dma((3, HALVES)), dma((3, HALVES, R)), dma((3, HALVES)), dma((3, HALVES))]
+            + [dma((3, HALVES)), dma((3, HALVES, R)), dma((3, HALVES)), dma((3, HALVES))] + [dma((3,))] * 2
             + [pltpu.SemaphoreType.REGULAR((3, HALVES))] * 2
         )
         y = pl.pallas_call(

time: 201 us -> 175 us (0.87)
  the two profiles are of different devices: /device:TPU:30 before, /device:TPU:0 now
where the time goes in v2:
time: 175 us
  Pallas kernels  171 us (98%)
  local copies, waits for them, and re-layouts  3 us (2%)
    pallas_call x1, Pallas kernels, step(): pl.pallas_call(functools.partial(kernel, R, parts, tile, top, names), out...  171 us

profile of v2, /device:TPU:0, one launch (start us, length us, event | category | flops | bytes accessed | tf_op | source)
XLA Modules:
  0.0 175.0 jit_solution(9866079696773071801)
XLA Ops:
  0.0 0.7 copy.31
  0.7 0.7 fusion.2
  1.4 0.6 select_maximum_fusion.refs_1_
  2.0 170.7 %moe.1 = bf16[256,2048]{1,0:T(8,128)(2,1)} custom-call(bf16[256,2048]{1,0:T(8,128)(2,1)} %bitcast.18, f32[16,256]{1,0:T(8,128)} %select_maximum_fusion.refs_1_, bf16[2048,1408]{1,0:T(8,128)(2,1)} %bitcast.14, bf16[2048,1408]{1,0:T(8,128)(2,1)} %bitcast.15, bf16[1408,2048]{1,0:T(8,128)(2,1)} %bitcast.16, bf16[2048,2816]{1,0:T(8,128)(2,1)} %refs_5_.1, ...), custom_call_target="tpu_custom_call" | custom-call | tf_op jit(solution)/shard_map/moe/pallas_call | solution.py:387
  172.7 2.3 %copy.33 = bf16[1,1,256,2048]{3,2,1,0:T(8,128)(2,1)} copy(bf16[1,1,256,2048]{3,2,1,0:T(8,128)(2,1)} %bitcast.17) | data formatting | bytes 2097152
  (1 shorter events, 0.0 us)

commit v3 on v2

--- a/solution.py
+++ b/solution.py
@@ -23,7 +23,7 @@
     (x_ref, m_ref, wg_hbm, wu_hbm, wd_hbm, sg_hbm, su_hbm, sd_hbm, y_ref) = refs[:9]
     xa, g_buf, h_buf, z_buf, ps = refs[9:12], refs[12:15], refs[15:18], refs[18:21], refs[21:24]
     (meta, wg, wu, wd, zcat, hb, yacc, sgb, sub, sdb,
-     w_sem, sh_sem, m_s, m_r, a_s, a_r, b_s, b_r, c_s, c_r, c2_s, c2_r, b2_s, b2_r, a2_s, a2_r, h_free, g_free) = refs[24:]
+     w_sem, sh_sem, m_s, m_r, a_s, a_r, b_s, b_r, c_s, c_r, c2_s, c2_r, b2_s, b2_r, a2_s, a2_r, ah_r, h_free, g_free) = refs[24:]
     dp_axis, ep_axis = names
     T = x_ref.shape[0]
     FF = wg.shape[1]
@@ -38,6 +38,8 @@
 
     order = sorted(range(3), key=lambda k: -parts[k])
     near = sorted(range(1, R), key=lambda r: (min(r, R - r), -r))
+    ring4 = R == 4
+    lo, hi = pl.ds(0, T // 2), pl.ds(T // 2, T // 2)
 
     def peer(axis, r):
         return me + (lax.rem(pos[axis] + r, R) - pos[axis]) * unit[axis]
@@ -149,12 +151,43 @@
         for r in near:
             send(m_ref, meta.at[k, R - r], m_s.at[k], m_r.at[k], k, r)
     for r in near:
-        for k in order:
-            send(x_ref.at[:, cols[k]], xa[k].at[R - r], a_s.at[k], a_r.at[k], k, r)
+        if not ring4 or r != 2:
+            for k in order:
+                send(x_ref.at[:, cols[k]], xa[k].at[R - r], a_s.at[k], a_r.at[k, R - r], k, r)
     for k in order:
         send_b(k, 0, 0)
 
-    pl.loop(0, n_sh - R)(jax.named_scope("shared")(shared))
+    early = max(n_sh - R - 2, 0)
+    pl.loop(0, early)(jax.named_scope("shared")(shared))
+
+    @jax.named_scope("wait_a")
+    def wait_a(k, ra):
+        pend(xa[k].at[ra], a_s.at[k], a_r.at[k, ra]).wait_recv()
+
+    @jax.named_scope("gather")
+    def gather_all(h, ra, go):
+        for k in order:
+            gather(k, h, ra, slot_ids(k, h))
+            if go:
+                send_b(k, h, ra)
+
+    for k in order:
+        with jax.named_scope("wait_m"):
+            pend(meta.at[k, 1:R], m_s.at[k], m_r.at[k]).wait_recv()
+    if ring4:
+        for k in order:
+            wait_a(k, 3)
+            send(xa[k].at[3, lo], xa[k].at[2, lo], a_s.at[k], a_r.at[k, 2], k, 1)
+            wait_a(k, 1)
+            send(xa[k].at[1, hi], xa[k].at[2, hi], a_s.at[k], a_r.at[k, 2], k, 3)
+        seq = [0, 3, 1, 2]
+
+        @pl.loop(0, 2)
+        def _(i):
+            gather_all(0, 3 - 2 * i, True)
+    else:
+        seq = list(range(R))
+    pl.loop(early, n_sh - R)(jax.named_scope("shared")(shared))
 
     w_copies = [
         pltpu.make_async_copy(src, dst, w_sem.at[i])
@@ -163,33 +196,25 @@
     for c in w_copies:
         c.start()
 
-    for k in order:
-        with jax.named_scope("wait_a"):
-            pend(meta.at[k, 1:R], m_s.at[k], m_r.at[k]).wait_recv()
-            pend(xa[k].at[1:R], a_s.at[k], a_r.at[k]).wait_recv()
-        ids = slot_ids(k, 0)
-
-        @pl.loop(1, R)
-        @jax.named_scope("gather")
-        def _(ra):
-            gather(k, 0, ra, ids)
-            send_b(k, 0, ra)
-
-    for k in order:
-        ids = slot_ids(k, 1)
-
-        @pl.loop(1, R)
-        @jax.named_scope("gather")
-        def _(ra):
-            gather(k, 1, ra, ids)
+    for ra in [2] if ring4 else seq[1:]:
+        for k in order:
+            wait_a(k, ra)
+        gather_all(0, ra, True)
+
+    @pl.loop(1, R)
+    def _(ra):
+        gather_all(1, ra, False)
 
     @pl.loop(0, R)
-    def _(ra):
+    def _(i):
         with jax.named_scope("shared"):
-            shared(n_sh - R + ra)
-        relay_c(0, ra)
-        for k in order:
-            send_b(k, 1, ra)
+            shared(n_sh - R + i)
+        for step, ra in enumerate(seq):
+            @pl.when(i == step)
+            def _():
+                relay_c(0, ra)
+                for k in order:
+                    send_b(k, 1, ra)
 
     for c in w_copies:
         c.wait()
@@ -245,6 +270,11 @@
         def _():
             for k in range(3):
                 pend(whole(k, h), c_s.at[k, h], c_r.at[k, h]).wait_recv()
+            @pl.when(t == 0)
+            def _():
+                for k in range(3):
+                    pend(xa[k].at[1:R], a_s.at[k], a2_r.at[k]).wait_send()
+
             for k in range(3):
                 pend(whole(k, h), c_s.at[k, h], c_r.at[k, h]).wait_send()
                 pend(whole(k, h), b_s.at[k, h], b_r.at[k, h]).wait_send()
@@ -254,8 +284,7 @@
 
         @pl.when(t == 0)
         def _():
-            @pl.loop(0, R // 2)
-            def _(ra):
+            for ra in seq[:R // 2]:
                 relay_c(1, ra)
 
         with jax.named_scope("up"):
@@ -279,8 +308,7 @@
 
         @pl.when(t == 0)
         def _():
-            @pl.loop(R // 2, R)
-            def _(ra):
+            for ra in seq[R // 2:]:
                 relay_c(1, ra)
 
         @pl.when(rx == R - 1)
@@ -294,13 +322,17 @@
     def own_rows(k, h):
         g_buf[k][h, 0, 0] = z_buf[k][(h,) + zsl(k, ALL, 0, 0)]
 
-    def weighted(k, ra, h):
-        ids = slot_ids(k, h)
-        w = jnp.zeros((KR, T), F32)
+    def weighted(k, ra, h, at=pl.ds(0, T)):
+        ids = slot_ids(k, h)[:, :at.size]
+        w = jnp.zeros((KR, at.size), F32)
         for j in range(top):
-            w += jnp.where(ids == meta[k, ra, j:j + 1, :], meta[k, ra, 8 + j:9 + j, :], 0.0)
+            gate = meta[k, ra, 8 + j:9 + j, at].astype(BF16).astype(F32)
+            w += jnp.where(ids == meta[k, ra, j:j + 1, at], gate, 0.0)
         rows = g_buf[k][h, :, :, ra].reshape(KR, parts[k])
         return lax.dot_general(w.astype(BF16), rows, (((0,), (0,)), ((), ())), preferred_element_type=F32)
+
+    def partial(k, ra, at=pl.ds(0, T)):
+        return weighted(k, ra, 0, at) + weighted(k, ra, 1, at)
 
     relay_b2(1)
     for k in order:
@@ -315,26 +347,48 @@
         with jax.named_scope("wait_b2"):
             pend(whole(k, 1), b2_s.at[k, 1], b2_r.at[k, 1]).wait_recv()
 
-        @pl.loop(1, R)
-        @jax.named_scope("weigh")
-        def _(ra):
-            ps[k][ra - 1] = (weighted(k, ra, 0) + weighted(k, ra, 1)).astype(BF16)
-            send(ps[k].at[ra - 1], xa[k].at[R - ra], a2_s.at[k], a2_r.at[k], k, ra)
+    def send_a2(k, ra, at):
+        send(ps[k].at[ra - 1, at], xa[k].at[R - ra, at], a2_s.at[k], a2_r.at[k], k, ra)
+
+    if ring4:
+        for k in order:
+            with jax.named_scope("weigh_far"):
+                ps[k][1] = partial(k, 2).astype(BF16)
+            send(ps[k].at[1, lo], xa[k].at[2, lo], a2_s.at[k], ah_r.at[k, 0], k, 1)
+            send(ps[k].at[1, hi], xa[k].at[2, hi], a2_s.at[k], ah_r.at[k, 1], k, 3)
+        for k in order:
+            with jax.named_scope("weigh_near"):
+                ps[k][0, hi] = partial(k, 1, hi).astype(BF16)
+                send_a2(k, 1, hi)
+                ps[k][2, lo] = partial(k, 3, lo).astype(BF16)
+                send_a2(k, 3, lo)
+        for k in order:
+            for i, (ra, at) in enumerate(((1, lo), (3, hi))):
+                with jax.named_scope("weigh_sum"):
+                    own = partial(k, ra, at)
+                    pend(xa[k].at[2, at], a2_s.at[k], ah_r.at[k, i]).wait_recv()
+                    ps[k][ra - 1, at] = (own + xa[k][2, at].astype(F32)).astype(BF16)
+                    send_a2(k, ra, at)
+    else:
+        for k in order:
+            for ra in range(1, R):
+                ps[k][ra - 1] = partial(k, ra).astype(BF16)
+                send_a2(k, ra, pl.ds(0, T))
+    senders = (1, 3) if ring4 else tuple(range(1, R))
 
     for k in order:
         with jax.named_scope("weigh_own"):
             yacc[:, cols[k]] += weighted(k, 0, 1)
     for k in order:
         with jax.named_scope("wait_a2"):
-            pend(xa[k].at[1:R], a2_s.at[k], a2_r.at[k]).wait_recv()
+            pend(xa[k].at[0:len(senders)], a2_s.at[k], a2_r.at[k]).wait_recv()
         total = yacc[:, cols[k]]
-        for ra in range(1, R):
+        for ra in senders:
             total += xa[k][ra].astype(F32)
         y_ref[:, cols[k]] = total.astype(BF16)
 
     for k in range(3):
         pend(meta.at[k, 1:R], m_s.at[k], m_r.at[k]).wait_send()
-        pend(xa[k].at[1:R], a_s.at[k], a_r.at[k]).wait_send()
         pend(xa[k].at[1:R], a2_s.at[k], a2_r.at[k]).wait_send()
         for h in range(HALVES):
             for s, r in ((c2_s, c2_r), (b2_s, b2_r)):
@@ -362,8 +416,7 @@
         parts = split(D)
         x, expert, slot, gate = x[0, 0], expert[0, 0], slot[0, 0], gate[0, 0]
         key = jnp.where(slot < slots, expert * SPAN + slot, -1).astype(F32)
-        weight = gate.astype(BF16).astype(F32)
-        m = jnp.concatenate([jnp.pad(key.T, ((0, 8 - top), (0, 0))), jnp.pad(weight.T, ((0, 8 - top), (0, 0)))], 0)
+        m = jnp.pad(key.T, ((0, 16 - top), (0, 0))) + jnp.pad(gate.T, ((8, 8 - top), (0, 0)))
         any_space = pl.BlockSpec(memory_space=pl.ANY)
         vmem = pl.BlockSpec(memory_space=pltpu.VMEM)
         tile = min(256, SFF)
@@ -379,9 +432,9 @@
             + [pltpu.VMEM((R * R * S, D), BF16), pltpu.VMEM((R * R * S, FF), BF16), pltpu.VMEM((T, D), F32)]
             + [pltpu.VMEM((2, D, tile), BF16), pltpu.VMEM((2, D, tile), BF16), pltpu.VMEM((2, tile, D), BF16)]
             + [dma((3,)), dma((2, 3))]
-            + [dma((3,))] * 4
+            + [dma((3,))] * 3 + [dma((3, R))]
             + [dma((3, HALVES)), dma((3, HALVES, R)), dma((3, HALVES)), dma((3, HALVES))]
-            + [dma((3, HALVES)), dma((3, HALVES, R)), dma((3, HALVES)), dma((3, HALVES))] + [dma((3,))] * 2
+            + [dma((3, HALVES)), dma((3, HALVES, R)), dma((3, HALVES)), dma((3, HALVES))] + [dma((3,))] * 2 + [dma((3, 2))]
             + [pltpu.SemaphoreType.REGULAR((3, HALVES))] * 2
         )
         y = pl.pallas_call(

time: 175 us -> 168 us (0.960)
  Pallas kernels: 171 us -> 163 us
    pallas_call x1, Pallas kernels: 171 us -> 163 us  [step(): pl.pallas_call(functools.partial(kernel, R, parts, tile, top, names), out...]
where the time goes in v3:
time: 168 us; the launch traced here: 167 us
  Pallas kernels  163 us (97%)
  local copies, waits for them, and re-layouts  3 us (2%)
    pallas_call x1, Pallas kernels, step(): pl.pallas_call(functools.partial(kernel, R, parts, tile, top, names), out...  163 us

profile of v3, /device:TPU:0, one launch (start us, length us, event | category | flops | bytes accessed | tf_op | source)
XLA Modules:
  0.0 167.5 jit_solution(15863831147228100532)
XLA Ops:
  0.0 0.7 fusion.2
  0.7 0.7 copy.29
  1.4 0.6 pad_add_fusion.refs_1_
  2.0 163.2 %moe.1 = bf16[256,2048]{1,0:T(8,128)(2,1)} custom-call(bf16[256,2048]{1,0:T(8,128)(2,1)} %bitcast.18, f32[16,256]{1,0:T(8,128)} %pad_add_fusion.refs_1_, bf16[2048,1408]{1,0:T(8,128)(2,1)} %bitcast.14, bf16[2048,1408]{1,0:T(8,128)(2,1)} %bitcast.15, bf16[1408,2048]{1,0:T(8,128)(2,1)} %bitcast.16, bf16[2048,2816]{1,0:T(8,128)(2,1)} %refs_5_.1, ...), custom_call_target="tpu_custom_call" | custom-call | tf_op jit(solution)/shard_map/moe/pallas_call | solution.py:440
  165.2 2.3 %copy.31 = bf16[1,1,256,2048]{3,2,1,0:T(8,128)(2,1)} copy(bf16[1,1,256,2048]{3,2,1,0:T(8,128)(2,1)} %bitcast.17) | data formatting | bytes 2097152

commit v4 on v3

--- a/solution.py
+++ b/solution.py
@@ -19,11 +19,11 @@
     return (jax.nn.silu(g) * u).astype(BF16)
 
 
-def kernel(R, parts, shared_tile, top, names, *refs):
-    (x_ref, m_ref, wg_hbm, wu_hbm, wd_hbm, sg_hbm, su_hbm, sd_hbm, y_ref) = refs[:9]
-    xa, g_buf, h_buf, z_buf, ps = refs[9:12], refs[12:15], refs[15:18], refs[18:21], refs[21:24]
-    (meta, wg, wu, wd, zcat, hb, yacc, sgb, sub, sdb,
-     w_sem, sh_sem, m_s, m_r, a_s, a_r, b_s, b_r, c_s, c_r, c2_s, c2_r, b2_s, b2_r, a2_s, a2_r, ah_r, h_free, g_free) = refs[24:]
+def kernel(R, parts, shared_tile, top, slots, names, *refs):
+    (x_ref, e_ref, s_ref, gate_ref, wg_hbm, wu_hbm, wd_hbm, sg_hbm, su_hbm, sd_hbm, y_ref) = refs[:11]
+    xa, g_buf, h_buf, z_buf, ps, own = (refs[i:i + 3] for i in range(11, 29, 3))
+    (m_ref, meta, wg, wu, wd, zcat, hb, yacc, sgb, sub, sdb,
+     w_sem, sh_sem, m_s, m_r, a_s, a_r, b_s, b_r, c_s, c_r, c2_s, c2_r, b2_s, b2_r, a2_s, a2_r, ah_r, h_free, g_free) = refs[29:]
     dp_axis, ep_axis = names
     T = x_ref.shape[0]
     FF = wg.shape[1]
@@ -133,6 +133,10 @@
         for r in range(1, R):
             pl.semaphore_signal(barrier, inc=1, device_id=(dp, peer(axis, r)), device_id_type=MESH)
 
+    m_ref[...] = jnp.zeros_like(m_ref)
+    for j in range(top):
+        m_ref[j:j + 1, :] = jnp.where(s_ref[j] < slots, e_ref[j] * SPAN + s_ref[j], -1).astype(F32)
+        m_ref[8 + j:9 + j, :] = gate_ref[j].astype(BF16).astype(F32)
     for k in range(3):
         meta[k, 0] = m_ref[...]
         xa[k][0] = x_ref[:, cols[k]]
@@ -322,27 +326,37 @@
     def own_rows(k, h):
         g_buf[k][h, 0, 0] = z_buf[k][(h,) + zsl(k, ALL, 0, 0)]
 
-    def weighted(k, ra, h, at=pl.ds(0, T)):
-        ids = slot_ids(k, h)[:, :at.size]
-        w = jnp.zeros((KR, at.size), F32)
-        for j in range(top):
-            gate = meta[k, ra, 8 + j:9 + j, at].astype(BF16).astype(F32)
-            w += jnp.where(ids == meta[k, ra, j:j + 1, at], gate, 0.0)
-        rows = g_buf[k][h, :, :, ra].reshape(KR, parts[k])
-        return lax.dot_general(w.astype(BF16), rows, (((0,), (0,)), ((), ())), preferred_element_type=F32)
-
-    def partial(k, ra, at=pl.ds(0, T)):
-        return weighted(k, ra, 0, at) + weighted(k, ra, 1, at)
+    wide_w = HALVES * KR
+    across = FF // wide_w
+
+    def block(k, ra):
+        i = k * R + ra
+        return pl.ds(i // across * T, T), pl.ds(i % across * wide_w, wide_w)
+
+    @jax.named_scope("weights")
+    def build(k, ra):
+        rows, columns = block(k, ra)
+        for h in range(HALVES):
+            ids = slot_ids(k, h)
+            w = jnp.zeros((KR, T), F32)
+            for j in range(top):
+                w += jnp.where(ids == meta[k, ra, j:j + 1, :], meta[k, ra, 8 + j:9 + j, :], 0.0)
+            wg[rows, pl.ds(columns.start + h * KR, KR)] = w.T.astype(BF16)
+
+    def partial(k, ra):
+        rows = g_buf[k][:, :, :, ra].reshape(wide_w, parts[k])
+        return jnp.dot(wg[block(k, ra)], rows, preferred_element_type=F32)
 
     relay_b2(1)
     for k in order:
         for h in range(HALVES):
             own_rows(k, h)
+    for ra in [2, 1, 3, 0] if ring4 else range(R):
+        for k in order:
+            build(k, ra)
     for k in order:
         with jax.named_scope("wait_b2"):
             pend(whole(k, 0), b2_s.at[k, 0], b2_r.at[k, 0]).wait_recv()
-        with jax.named_scope("weigh_own"):
-            yacc[:, cols[k]] += weighted(k, 0, 0)
     for k in order:
         with jax.named_scope("wait_b2"):
             pend(whole(k, 1), b2_s.at[k, 1], b2_r.at[k, 1]).wait_recv()
@@ -358,16 +372,16 @@
             send(ps[k].at[1, hi], xa[k].at[2, hi], a2_s.at[k], ah_r.at[k, 1], k, 3)
         for k in order:
             with jax.named_scope("weigh_near"):
-                ps[k][0, hi] = partial(k, 1, hi).astype(BF16)
-                send_a2(k, 1, hi)
-                ps[k][2, lo] = partial(k, 3, lo).astype(BF16)
-                send_a2(k, 3, lo)
+                for i, (ra, now, later) in enumerate(((1, slice(T // 2, T), slice(0, T // 2)), (3, slice(0, T // 2), slice(T // 2, T)))):
+                    p = partial(k, ra)
+                    ps[k][ra - 1, now] = p[now].astype(BF16)
+                    send_a2(k, ra, hi if i == 0 else lo)
+                    own[k][i] = p[later]
         for k in order:
             for i, (ra, at) in enumerate(((1, lo), (3, hi))):
                 with jax.named_scope("weigh_sum"):
-                    own = partial(k, ra, at)
                     pend(xa[k].at[2, at], a2_s.at[k], ah_r.at[k, i]).wait_recv()
-                    ps[k][ra - 1, at] = (own + xa[k][2, at].astype(F32)).astype(BF16)
+                    ps[k][ra - 1, at] = (own[k][i] + xa[k][2, at].astype(F32)).astype(BF16)
                     send_a2(k, ra, at)
     else:
         for k in order:
@@ -378,7 +392,7 @@
 
     for k in order:
         with jax.named_scope("weigh_own"):
-            yacc[:, cols[k]] += weighted(k, 0, 1)
+            yacc[:, cols[k]] += partial(k, 0)
     for k in order:
         with jax.named_scope("wait_a2"):
             pend(xa[k].at[0:len(senders)], a2_s.at[k], a2_r.at[k]).wait_recv()
@@ -414,9 +428,7 @@
         FF, SFF = w_gate.shape[-1], s_gate.shape[-1]
         slots = 5 * T * top // (4 * members)
         parts = split(D)
-        x, expert, slot, gate = x[0, 0], expert[0, 0], slot[0, 0], gate[0, 0]
-        key = jnp.where(slot < slots, expert * SPAN + slot, -1).astype(F32)
-        m = jnp.pad(key.T, ((0, 16 - top), (0, 0))) + jnp.pad(gate.T, ((8, 8 - top), (0, 0)))
+        x, (expert, slot, gate) = x[0, 0], (v[0].transpose(2, 0, 1) for v in (expert, slot, gate))
         any_space = pl.BlockSpec(memory_space=pl.ANY)
         vmem = pl.BlockSpec(memory_space=pltpu.VMEM)
         tile = min(256, SFF)
@@ -427,7 +439,8 @@
             + [pltpu.VMEM((HALVES, R - 1, R, R, S, c), BF16) for c in parts]
             + [pltpu.VMEM((HALVES, R, R, R, S, c), BF16) for c in parts]
             + [pltpu.VMEM((R - 1, T, c), BF16) for c in parts]
-            + [pltpu.VMEM((3, R, 16, T), F32)]
+            + [pltpu.VMEM((2, T // 2, c), F32) for c in parts]
+            + [pltpu.VMEM((16, T), F32), pltpu.VMEM((3, R, 16, T), F32)]
             + [pltpu.VMEM((D, FF), BF16), pltpu.VMEM((D, FF), BF16), pltpu.VMEM((FF, D), BF16)]
             + [pltpu.VMEM((R * R * S, D), BF16), pltpu.VMEM((R * R * S, FF), BF16), pltpu.VMEM((T, D), F32)]
             + [pltpu.VMEM((2, D, tile), BF16), pltpu.VMEM((2, D, tile), BF16), pltpu.VMEM((2, tile, D), BF16)]
@@ -438,16 +451,16 @@
             + [pltpu.SemaphoreType.REGULAR((3, HALVES))] * 2
         )
         y = pl.pallas_call(
-            functools.partial(kernel, R, parts, tile, top, names),
+            functools.partial(kernel, R, parts, tile, top, slots, names),
             out_shape=jax.ShapeDtypeStruct((T, D), BF16),
-            in_specs=[vmem, vmem] + [any_space] * 6,
+            in_specs=[vmem] * 4 + [any_space] * 6,
             out_specs=vmem,
             scratch_shapes=scratch,
             compiler_params=pltpu.CompilerParams(
                 collective_id=0, has_side_effects=True, vmem_limit_bytes=67043328
             ),
             name="moe",
-        )(x, m, w_gate[0], w_up[0], w_down[0], s_gate, s_up, s_down)
+        )(x, expert, slot, gate, w_gate[0], w_up[0], w_down[0], s_gate, s_up, s_down)
         return y[None, None]
 
     tok = P("dp", "ep", None, None)

time: 168 us -> 165 us (0.982)
  no operation moved by 1% of the time
where the time goes in v4:
time: 165 us
  Pallas kernels  162 us (98%)
  local copies, waits for them, and re-layouts  2.3 us (1%)
    pallas_call x1, Pallas kernels, step(): pl.pallas_call(functools.partial(kernel, R, parts, tile, top, slots, name...  162 us

profile of v4, /device:TPU:0, one launch (start us, length us, event | category | flops | bytes accessed | tf_op | source)
XLA Modules:
  0.0 164.5 jit_solution(15195615130764621977)
XLA Ops:
  0.0 162.2 %moe.1 = bf16[256,2048]{1,0:T(8,128)(2,1)} custom-call(bf16[256,2048]{1,0:T(8,128)(2,1)} %bitcast.18, s32[6,1,256]{2,1,0:T(1,128)} %bitcast.19, s32[6,1,256]{2,1,0:T(1,128)} %bitcast.20, f32[6,1,256]{2,1,0:T(1,128)} %bitcast.21, bf16[2048,1408]{1,0:T(8,128)(2,1)} %bitcast.14, bf16[2048,1408]{1,0:T(8,128)(2,1)} %bitcast.15, bf16[1408,2048]{1,0:T(8,128)(2,1)} %bitcast.16, ...), custom_call_target="tpu_custom_call" | custom-call | tf_op jit(solution)/shard_map/moe/pallas_call | solution.py:453
  162.2 2.3 %copy.12 = bf16[1,1,256,2048]{3,2,1,0:T(8,128)(2,1)} copy(bf16[1,1,256,2048]{3,2,1,0:T(8,128)(2,1)} %bitcast.17) | data formatting | bytes 2097152

commit v5 on v4

--- a/solution.py
+++ b/solution.py
@@ -20,10 +20,10 @@
 
 
 def kernel(R, parts, shared_tile, top, slots, names, *refs):
-    (x_ref, e_ref, s_ref, gate_ref, wg_hbm, wu_hbm, wd_hbm, sg_hbm, su_hbm, sd_hbm, y_ref) = refs[:11]
-    xa, g_buf, h_buf, z_buf, ps, own = (refs[i:i + 3] for i in range(11, 29, 3))
-    (m_ref, meta, wg, wu, wd, zcat, hb, yacc, sgb, sub, sdb,
-     w_sem, sh_sem, m_s, m_r, a_s, a_r, b_s, b_r, c_s, c_r, c2_s, c2_r, b2_s, b2_r, a2_s, a2_r, ah_r, h_free, g_free) = refs[29:]
+    (x_hbm, e_hbm, s_hbm, gate_hbm, wg_hbm, wu_hbm, wd_hbm, sg_hbm, su_hbm, sd_hbm, y_ref) = refs[:11]
+    xa, g_buf, h_buf, z_buf, own = (refs[i:i + 3] for i in range(11, 26, 3))
+    (x_ref, e_ref, s_ref, gate_ref, m_ref, meta, wg, wu, wd, zcat, hb, yacc, sgb, sub, sdb,
+     in_sem, w_sem, sh_sem, m_s, m_r, a_s, a_r, b_s, b_r, c_s, c_r, c2_s, c2_r, b2_s, b2_r, a2_s, a2_r, ah_r, h_free, g_free) = refs[26:]
     dp_axis, ep_axis = names
     T = x_ref.shape[0]
     FF = wg.shape[1]
@@ -77,7 +77,11 @@
             pltpu.make_async_copy(sd_hbm.at[at], sdb.at[slot], sh_sem.at[slot, 2]),
         )
 
-    for c in sh_copies(0, 0):
+    in_copies = [
+        pltpu.make_async_copy(src, dst, in_sem.at[i])
+        for i, (src, dst) in enumerate(((x_hbm, x_ref), (e_hbm, e_ref), (s_hbm, s_ref), (gate_hbm, gate_ref)))
+    ]
+    for c in in_copies:
         c.start()
 
     def shared(j):
@@ -133,21 +137,15 @@
         for r in range(1, R):
             pl.semaphore_signal(barrier, inc=1, device_id=(dp, peer(axis, r)), device_id_type=MESH)
 
+    for c in sh_copies(0, 0):
+        c.start()
+    for c in in_copies[1:]:
+        c.wait()
     m_ref[...] = jnp.zeros_like(m_ref)
     for j in range(top):
         m_ref[j:j + 1, :] = jnp.where(s_ref[j] < slots, e_ref[j] * SPAN + s_ref[j], -1).astype(F32)
         m_ref[8 + j:9 + j, :] = gate_ref[j].astype(BF16).astype(F32)
-    for k in range(3):
-        meta[k, 0] = m_ref[...]
-        xa[k][0] = x_ref[:, cols[k]]
-    yacc[...] = jnp.zeros_like(yacc)
-
-    @pl.loop(0, HALVES)
-    @jax.named_scope("gather")
-    def _(h):
-        for k in order:
-            gather(k, h, 0, slot_ids(k, h))
-
+    in_copies[0].wait()
     with jax.named_scope("barrier"):
         pl.semaphore_wait(barrier, 3 * (R - 1))
 
@@ -158,8 +156,13 @@
         if not ring4 or r != 2:
             for k in order:
                 send(x_ref.at[:, cols[k]], xa[k].at[R - r], a_s.at[k], a_r.at[k, R - r], k, r)
-    for k in order:
+    for k in range(3):
+        meta[k, 0] = m_ref[...]
+        xa[k][0] = x_ref[:, cols[k]]
+    for k in order:
+        gather(k, 0, 0, slot_ids(k, 0))
         send_b(k, 0, 0)
+    yacc[...] = jnp.zeros_like(yacc)
 
     early = max(n_sh - R - 2, 0)
     pl.loop(0, early)(jax.named_scope("shared")(shared))
@@ -205,7 +208,7 @@
             wait_a(k, ra)
         gather_all(0, ra, True)
 
-    @pl.loop(1, R)
+    @pl.loop(0, R)
     def _(ra):
         gather_all(1, ra, False)
 
@@ -361,32 +364,38 @@
         with jax.named_scope("wait_b2"):
             pend(whole(k, 1), b2_s.at[k, 1], b2_r.at[k, 1]).wait_recv()
 
+    def ps(k, ra, at):
+        beside = k == 2 and parts[0] + parts[2] <= FF
+        row = ((0 if beside else k) * (R - 1) + ra - 1) * T + at.start
+        left = parts[0] if beside else 0
+        return wu.at[pl.ds(row, at.size), pl.ds(left, parts[k])]
+
     def send_a2(k, ra, at):
-        send(ps[k].at[ra - 1, at], xa[k].at[R - ra, at], a2_s.at[k], a2_r.at[k], k, ra)
+        send(ps(k, ra, at), xa[k].at[R - ra, at], a2_s.at[k], a2_r.at[k], k, ra)
 
     if ring4:
         for k in order:
             with jax.named_scope("weigh_far"):
-                ps[k][1] = partial(k, 2).astype(BF16)
-            send(ps[k].at[1, lo], xa[k].at[2, lo], a2_s.at[k], ah_r.at[k, 0], k, 1)
-            send(ps[k].at[1, hi], xa[k].at[2, hi], a2_s.at[k], ah_r.at[k, 1], k, 3)
+                ps(k, 2, pl.ds(0, T))[...] = partial(k, 2).astype(BF16)
+            send(ps(k, 2, lo), xa[k].at[2, lo], a2_s.at[k], ah_r.at[k, 0], k, 1)
+            send(ps(k, 2, hi), xa[k].at[2, hi], a2_s.at[k], ah_r.at[k, 1], k, 3)
         for k in order:
             with jax.named_scope("weigh_near"):
-                for i, (ra, now, later) in enumerate(((1, slice(T // 2, T), slice(0, T // 2)), (3, slice(0, T // 2), slice(T // 2, T)))):
+                for i, (ra, now, later) in enumerate(((1, hi, lo), (3, lo, hi))):
                     p = partial(k, ra)
-                    ps[k][ra - 1, now] = p[now].astype(BF16)
-                    send_a2(k, ra, hi if i == 0 else lo)
-                    own[k][i] = p[later]
+                    ps(k, ra, now)[...] = p[now.start:now.start + now.size].astype(BF16)
+                    send_a2(k, ra, now)
+                    own[k][i] = p[later.start:later.start + later.size]
         for k in order:
             for i, (ra, at) in enumerate(((1, lo), (3, hi))):
                 with jax.named_scope("weigh_sum"):
                     pend(xa[k].at[2, at], a2_s.at[k], ah_r.at[k, i]).wait_recv()
-                    ps[k][ra - 1, at] = (own[k][i] + xa[k][2, at].astype(F32)).astype(BF16)
+                    ps(k, ra, at)[...] = (own[k][i] + xa[k][2, at].astype(F32)).astype(BF16)
                     send_a2(k, ra, at)
     else:
         for k in order:
             for ra in range(1, R):
-                ps[k][ra - 1] = partial(k, ra).astype(BF16)
+                ps(k, ra, pl.ds(0, T))[...] = partial(k, ra).astype(BF16)
                 send_a2(k, ra, pl.ds(0, T))
     senders = (1, 3) if ring4 else tuple(range(1, R))
 
@@ -438,13 +447,14 @@
             + [pltpu.VMEM((HALVES, R, R, R, S, c), BF16) for c in parts]
             + [pltpu.VMEM((HALVES, R - 1, R, R, S, c), BF16) for c in parts]
             + [pltpu.VMEM((HALVES, R, R, R, S, c), BF16) for c in parts]
-            + [pltpu.VMEM((R - 1, T, c), BF16) for c in parts]
             + [pltpu.VMEM((2, T // 2, c), F32) for c in parts]
+            + [pltpu.VMEM((T, D), BF16), pltpu.VMEM((top, 1, T), jnp.int32), pltpu.VMEM((top, 1, T), jnp.int32),
+               pltpu.VMEM((top, 1, T), F32)]
             + [pltpu.VMEM((16, T), F32), pltpu.VMEM((3, R, 16, T), F32)]
             + [pltpu.VMEM((D, FF), BF16), pltpu.VMEM((D, FF), BF16), pltpu.VMEM((FF, D), BF16)]
             + [pltpu.VMEM((R * R * S, D), BF16), pltpu.VMEM((R * R * S, FF), BF16), pltpu.VMEM((T, D), F32)]
             + [pltpu.VMEM((2, D, tile), BF16), pltpu.VMEM((2, D, tile), BF16), pltpu.VMEM((2, tile, D), BF16)]
-            + [dma((3,)), dma((2, 3))]
+            + [dma((4,)), dma((3,)), dma((2, 3))]
             + [dma((3,))] * 3 + [dma((3, R))]
             + [dma((3, HALVES)), dma((3, HALVES, R)), dma((3, HALVES)), dma((3, HALVES))]
             + [dma((3, HALVES)), dma((3, HALVES, R)), dma((3, HALVES)), dma((3, HALVES))] + [dma((3,))] * 2 + [dma((3, 2))]
@@ -453,7 +463,7 @@
         y = pl.pallas_call(
             functools.partial(kernel, R, parts, tile, top, slots, names),
             out_shape=jax.ShapeDtypeStruct((T, D), BF16),
-            in_specs=[vmem] * 4 + [any_space] * 6,
+            in_specs=[any_space] * 10,
             out_specs=vmem,
             scratch_shapes=scratch,
             compiler_params=pltpu.CompilerParams(

time: 165 us -> 163 us (0.988)
  Pallas kernels: 162 us -> 160 us
    pallas_call x1, Pallas kernels: 162 us -> 160 us  [step(): pl.pallas_call(functools.partial(kernel, R, parts, tile, top, slots, name...]
where the time goes in v5:
time: 163 us
  Pallas kernels  160 us (98%)
  local copies, waits for them, and re-layouts  2.3 us (1%)
    pallas_call x1, Pallas kernels, step(): pl.pallas_call(functools.partial(kernel, R, parts, tile, top, slots, name...  160 us

profile of v5, /device:TPU:0, one launch (start us, length us, event | category | flops | bytes accessed | tf_op | source)
XLA Modules:
  0.0 162.6 jit_solution(10766272678371882550)
XLA Ops:
  0.0 160.3 %moe.1 = bf16[256,2048]{1,0:T(8,128)(2,1)} custom-call(bf16[256,2048]{1,0:T(8,128)(2,1)} %bitcast.18, s32[6,1,256]{2,1,0:T(1,128)} %bitcast.19, s32[6,1,256]{2,1,0:T(1,128)} %bitcast.20, f32[6,1,256]{2,1,0:T(1,128)} %bitcast.21, bf16[2048,1408]{1,0:T(8,128)(2,1)} %bitcast.14, bf16[2048,1408]{1,0:T(8,128)(2,1)} %bitcast.15, bf16[1408,2048]{1,0:T(8,128)(2,1)} %bitcast.16, ...), custom_call_target="tpu_custom_call" | custom-call | tf_op jit(solution)/shard_map/moe/pallas_call | solution.py:463
  160.3 2.3 %copy.12 = bf16[1,1,256,2048]{3,2,1,0:T(8,128)(2,1)} copy(bf16[1,1,256,2048]{3,2,1,0:T(8,128)(2,1)} %bitcast.17) | data formatting | bytes 2097152

commit v6 on v5

--- a/solution.py
+++ b/solution.py
@@ -20,10 +20,10 @@
 
 
 def kernel(R, parts, shared_tile, top, slots, names, *refs):
-    (x_hbm, e_hbm, s_hbm, gate_hbm, wg_hbm, wu_hbm, wd_hbm, sg_hbm, su_hbm, sd_hbm, y_ref) = refs[:11]
+    (x_hbm, e_hbm, s_hbm, gate_hbm, wg_hbm, wu_hbm, wd_hbm, sg_hbm, su_hbm, sd_hbm, y_hbm) = refs[:11]
     xa, g_buf, h_buf, z_buf, own = (refs[i:i + 3] for i in range(11, 26, 3))
-    (x_ref, e_ref, s_ref, gate_ref, m_ref, meta, wg, wu, wd, zcat, hb, yacc, sgb, sub, sdb,
-     in_sem, w_sem, sh_sem, m_s, m_r, a_s, a_r, b_s, b_r, c_s, c_r, c2_s, c2_r, b2_s, b2_r, a2_s, a2_r, ah_r, h_free, g_free) = refs[26:]
+    (y_ref, x_ref, e_ref, s_ref, gate_ref, m_ref, meta, wg, wu, wd, zcat, hb, yacc, sgb, sub, sdb,
+     out_sem, in_sem, w_sem, sh_sem, m_s, m_r, a_s, a_r, b_s, b_r, c_s, c_r, c2_s, c2_r, b2_s, b2_r, a2_s, a2_r, ah_r, h_free, g_free) = refs[26:]
     dp_axis, ep_axis = names
     T = x_ref.shape[0]
     FF = wg.shape[1]
@@ -39,6 +39,7 @@
     order = sorted(range(3), key=lambda k: -parts[k])
     near = sorted(range(1, R), key=lambda r: (min(r, R - r), -r))
     ring4 = R == 4
+    back = (0, 2, 1)
     lo, hi = pl.ds(0, T // 2), pl.ds(T // 2, T // 2)
 
     def peer(axis, r):
@@ -225,16 +226,18 @@
 
     for c in w_copies:
         c.wait()
+    for ra in seq[:-1]:
+        relay_c(1, ra)
 
     def send_c2(h, rx):
         for k in order:
-            s, axis = c2_s.at[k, h], (k + 2) % 3
+            s, axis = c2_s.at[k, h], (back[k] + 2) % 3
             z, hh, g = z_buf[k], h_buf[k], g_buf[k]
-            if k == 0:
+            if back[k] == 0:
                 for rc in near:
                     send(z.at[h, rx, 1:R, rc], hh.at[h, R - rc - 1, rx, 1:R], s, c2_r.at[k, h, R - rc], axis, rc)
                     send(z.at[h, rx, 0, rc], g.at[h, 0, R - rc, rx], s, c2_r.at[k, h, R - rc], axis, rc)
-            elif k == 1:
+            elif back[k] == 1:
                 @pl.when(rx > 0)
                 def _():
                     send(z.at[h, rx, :, 1:R], hh.at[h, R - rx - 1, :, 1:R], s, c2_r.at[k, h, R - rx], axis, rx)
@@ -254,8 +257,8 @@
         for k in order:
             pl.semaphore_wait(g_free.at[k, h], R - 1)
             for rb in near:
-                send(z_buf[k].at[(h,) + zsl(k, ALL, rb, 0)], g_buf[k].at[h, R - rb, 0],
-                     b2_s.at[k, h], b2_r.at[k, h], (k + 1) % 3, rb)
+                send(z_buf[k].at[(h,) + zsl(back[k], ALL, rb, 0)], g_buf[k].at[h, R - rb, 0],
+                     b2_s.at[k, h], b2_r.at[k, h], (back[k] + 1) % 3, rb)
 
     @jax.named_scope("relay_b2")
     def relay_b2(h):
@@ -263,8 +266,8 @@
             for k in order:
                 pend(g_buf[k].at[h, 1], c2_s.at[k, h], c2_r.at[k, h, ce]).wait_recv()
                 for rb in near:
-                    send(h_buf[k].at[(h, ce - 1) + hsl(k, ALL, rb)], g_buf[k].at[h, R - rb, ce],
-                         b2_s.at[k, h], b2_r.at[k, h], (k + 1) % 3, rb)
+                    send(h_buf[k].at[(h, ce - 1) + hsl(back[k], ALL, rb)], g_buf[k].at[h, R - rb, ce],
+                         b2_s.at[k, h], b2_r.at[k, h], (back[k] + 1) % 3, rb)
 
     wide = [(n, min(512, FF - n)) for n in range(0, FF, 512)]
 
@@ -285,14 +288,9 @@
             for k in range(3):
                 pend(whole(k, h), c_s.at[k, h], c_r.at[k, h]).wait_send()
                 pend(whole(k, h), b_s.at[k, h], b_r.at[k, h]).wait_send()
-                for free, axis in ((h_free, k + 2), (g_free, k + 1)):
+                for free, axis in ((h_free, back[k] + 2), (g_free, back[k] + 1)):
                     for r in range(1, R):
                         pl.semaphore_signal(free.at[k, h], inc=1, device_id=(dp, peer(axis % 3, r)), device_id_type=MESH)
-
-        @pl.when(t == 0)
-        def _():
-            for ra in seq[:R // 2]:
-                relay_c(1, ra)
 
         with jax.named_scope("up"):
             for k in range(3):
@@ -315,19 +313,18 @@
 
         @pl.when(t == 0)
         def _():
-            for ra in seq[R // 2:]:
-                relay_c(1, ra)
+            relay_c(1, seq[-1])
 
         @pl.when(rx == R - 1)
         def _():
             own_b2(h)
 
-        @pl.when(t == R + R // 2 - 1)
+        @pl.when(t == R)
         def _():
             relay_b2(0)
 
     def own_rows(k, h):
-        g_buf[k][h, 0, 0] = z_buf[k][(h,) + zsl(k, ALL, 0, 0)]
+        g_buf[k][h, 0, 0] = z_buf[k][(h,) + zsl(back[k], ALL, 0, 0)]
 
     wide_w = HALVES * KR
     across = FF // wide_w
@@ -340,10 +337,10 @@
     def build(k, ra):
         rows, columns = block(k, ra)
         for h in range(HALVES):
-            ids = slot_ids(k, h)
+            ids = slot_ids(back[k], h)
             w = jnp.zeros((KR, T), F32)
             for j in range(top):
-                w += jnp.where(ids == meta[k, ra, j:j + 1, :], meta[k, ra, 8 + j:9 + j, :], 0.0)
+                w += jnp.where(ids == meta[back[k], ra, j:j + 1, :], meta[back[k], ra, 8 + j:9 + j, :], 0.0)
             wg[rows, pl.ds(columns.start + h * KR, KR)] = w.T.astype(BF16)
 
     def partial(k, ra):
@@ -371,14 +368,14 @@
         return wu.at[pl.ds(row, at.size), pl.ds(left, parts[k])]
 
     def send_a2(k, ra, at):
-        send(ps(k, ra, at), xa[k].at[R - ra, at], a2_s.at[k], a2_r.at[k], k, ra)
+        send(ps(k, ra, at), xa[k].at[R - ra, at], a2_s.at[k], a2_r.at[k], back[k], ra)
 
     if ring4:
         for k in order:
             with jax.named_scope("weigh_far"):
                 ps(k, 2, pl.ds(0, T))[...] = partial(k, 2).astype(BF16)
-            send(ps(k, 2, lo), xa[k].at[2, lo], a2_s.at[k], ah_r.at[k, 0], k, 1)
-            send(ps(k, 2, hi), xa[k].at[2, hi], a2_s.at[k], ah_r.at[k, 1], k, 3)
+            send(ps(k, 2, lo), xa[k].at[2, lo], a2_s.at[k], ah_r.at[k, 0], back[k], 1)
+            send(ps(k, 2, hi), xa[k].at[2, hi], a2_s.at[k], ah_r.at[k, 1], back[k], 3)
         for k in order:
             with jax.named_scope("weigh_near"):
                 for i, (ra, now, later) in enumerate(((1, hi, lo), (3, lo, hi))):
@@ -409,13 +406,29 @@
         for ra in senders:
             total += xa[k][ra].astype(F32)
         y_ref[:, cols[k]] = total.astype(BF16)
+        pltpu.make_async_copy(y_ref.at[:, cols[k]], y_hbm.at[:, cols[k]], out_sem.at[k]).start()
 
     for k in range(3):
+        pltpu.make_async_copy(y_ref.at[:, cols[k]], y_hbm.at[:, cols[k]], out_sem.at[k]).wait()
         pend(meta.at[k, 1:R], m_s.at[k], m_r.at[k]).wait_send()
         pend(xa[k].at[1:R], a2_s.at[k], a2_r.at[k]).wait_send()
         for h in range(HALVES):
             for s, r in ((c2_s, c2_r), (b2_s, b2_r)):
                 pend(whole(k, h), s.at[k, h], r.at[k, h]).wait_send()
+
+
+def hand_on(pieces, src, dst, held, in_sem, out_sem):
+    n = src.shape[0] // pieces
+    rows = [pl.ds(i * n, n) for i in range(pieces)]
+    into = [pltpu.make_async_copy(src.at[r], held.at[r], in_sem.at[i]) for i, r in enumerate(rows)]
+    out = [pltpu.make_async_copy(held.at[r], dst.at[r], out_sem.at[i]) for i, r in enumerate(rows)]
+    for c in into:
+        c.start()
+    for a, b in zip(into, out):
+        a.wait()
+        b.start()
+    for c in out:
+        c.wait()
 
 
 def split(d):
@@ -439,7 +452,6 @@
         parts = split(D)
         x, (expert, slot, gate) = x[0, 0], (v[0].transpose(2, 0, 1) for v in (expert, slot, gate))
         any_space = pl.BlockSpec(memory_space=pl.ANY)
-        vmem = pl.BlockSpec(memory_space=pltpu.VMEM)
         tile = min(256, SFF)
         dma = pltpu.SemaphoreType.DMA
         scratch = (
@@ -448,13 +460,13 @@
             + [pltpu.VMEM((HALVES, R - 1, R, R, S, c), BF16) for c in parts]
             + [pltpu.VMEM((HALVES, R, R, R, S, c), BF16) for c in parts]
             + [pltpu.VMEM((2, T // 2, c), F32) for c in parts]
-            + [pltpu.VMEM((T, D), BF16), pltpu.VMEM((top, 1, T), jnp.int32), pltpu.VMEM((top, 1, T), jnp.int32),
+            + [pltpu.VMEM((T, D), BF16), pltpu.VMEM((T, D), BF16), pltpu.VMEM((top, 1, T), jnp.int32), pltpu.VMEM((top, 1, T), jnp.int32),
                pltpu.VMEM((top, 1, T), F32)]
             + [pltpu.VMEM((16, T), F32), pltpu.VMEM((3, R, 16, T), F32)]
             + [pltpu.VMEM((D, FF), BF16), pltpu.VMEM((D, FF), BF16), pltpu.VMEM((FF, D), BF16)]
             + [pltpu.VMEM((R * R * S, D), BF16), pltpu.VMEM((R * R * S, FF), BF16), pltpu.VMEM((T, D), F32)]
             + [pltpu.VMEM((2, D, tile), BF16), pltpu.VMEM((2, D, tile), BF16), pltpu.VMEM((2, tile, D), BF16)]
-            + [dma((4,)), dma((3,)), dma((2, 3))]
+            + [dma((3,)), dma((4,)), dma((3,)), dma((2, 3))]
             + [dma((3,))] * 3 + [dma((3, R))]
             + [dma((3, HALVES)), dma((3, HALVES, R)), dma((3, HALVES)), dma((3, HALVES))]
             + [dma((3, HALVES)), dma((3, HALVES, R)), dma((3, HALVES)), dma((3, HALVES))] + [dma((3,))] * 2 + [dma((3, 2))]
@@ -464,13 +476,22 @@
             functools.partial(kernel, R, parts, tile, top, slots, names),
             out_shape=jax.ShapeDtypeStruct((T, D), BF16),
             in_specs=[any_space] * 10,
-            out_specs=vmem,
+            out_specs=any_space,
             scratch_shapes=scratch,
             compiler_params=pltpu.CompilerParams(
                 collective_id=0, has_side_effects=True, vmem_limit_bytes=67043328
             ),
             name="moe",
         )(x, expert, slot, gate, w_gate[0], w_up[0], w_down[0], s_gate, s_up, s_down)
+        pieces = 8
+        y = pl.pallas_call(
+            functools.partial(hand_on, pieces),
+            out_shape=jax.ShapeDtypeStruct((T, D), BF16),
+            in_specs=[any_space],
+            out_specs=any_space,
+            scratch_shapes=[pltpu.VMEM((T, D), BF16), dma((pieces,)), dma((pieces,))],
+            name="hand_on",
+        )(y)
         return y[None, None]
 
     tok = P("dp", "ep", None, None)

time: 163 us -> 163 us (level)
  Pallas kernels: 160 us -> 163 us
  local copies, waits for them, and re-layouts: 2.3 us -> 0 us
    unnamed x1 -> x0, local copies, waits for them, and re-layouts: 2.3 us -> none
    pallas_call x0 -> x1, Pallas kernels: none -> 2.09 us  [step(): pl.pallas_call(functools.partial(hand_on, pieces), out_shape=jax.ShapeDty...]
where the time goes in v6:
time: 163 us
  Pallas kernels  163 us (100%)
    pallas_call x1, Pallas kernels, step(): pl.pallas_call(functools.partial(kernel, R, parts, tile, top, slots, name...  161 us

profile of v6, /device:TPU:0, one launch (start us, length us, event | category | flops | bytes accessed | tf_op | source)
XLA Modules:
  0.0 162.9 jit_solution(15521129612081005073)
XLA Ops:
  0.0 160.7 %moe.1.src = bf16[256,2048]{1,0:T(8,128)(2,1)} custom-call(bf16[256,2048]{1,0:T(8,128)(2,1)} %bitcast.17, s32[6,1,256]{2,1,0:T(1,128)} %bitcast.18, s32[6,1,256]{2,1,0:T(1,128)} %bitcast.19, f32[6,1,256]{2,1,0:T(1,128)} %bitcast.20, bf16[2048,1408]{1,0:T(8,128)(2,1)} %bitcast.14, bf16[2048,1408]{1,0:T(8,128)(2,1)} %bitcast.15, bf16[1408,2048]{1,0:T(8,128)(2,1)} %bitcast.16, ...), custom_call_target="tpu_custom_call" | custom-call | tf_op jit(solution)/shard_map/moe/pallas_call | solution.py:475
  160.7 2.1 %hand_on.1 = bf16[256,2048]{1,0:T(8,128)(2,1)} custom-call(bf16[256,2048]{1,0:T(8,128)(2,1)} %moe.1.src), custom_call_target="tpu_custom_call" | custom-call | tf_op jit(solution)/shard_map/hand_on/pallas_call | solution.py:487

commit v7 on v6

--- a/solution.py
+++ b/solution.py
@@ -153,24 +153,25 @@
     for k in order:
         for r in near:
             send(m_ref, meta.at[k, R - r], m_s.at[k], m_r.at[k], k, r)
-    for r in near:
-        if not ring4 or r != 2:
+    halves = {1: (lo, hi), 3: (hi, lo)} if ring4 else {r: (lo, hi) for r in near}
+    for i in range(2):
+        for r in halves:
+            at = halves[r][i]
             for k in order:
-                send(x_ref.at[:, cols[k]], xa[k].at[R - r], a_s.at[k], a_r.at[k, R - r], k, r)
+                send(x_ref.at[at, cols[k]], xa[k].at[R - r, at], a_s.at[k], a_r.at[k, R - r, i], k, r)
     for k in range(3):
         meta[k, 0] = m_ref[...]
         xa[k][0] = x_ref[:, cols[k]]
+    yacc[...] = jnp.zeros_like(yacc)
     for k in order:
         gather(k, 0, 0, slot_ids(k, 0))
-        send_b(k, 0, 0)
-    yacc[...] = jnp.zeros_like(yacc)
-
-    early = max(n_sh - R - 2, 0)
-    pl.loop(0, early)(jax.named_scope("shared")(shared))
+
+    late = 2 * R - 1
+    early = max(n_sh - late, 0)
 
     @jax.named_scope("wait_a")
-    def wait_a(k, ra):
-        pend(xa[k].at[ra], a_s.at[k], a_r.at[k, ra]).wait_recv()
+    def wait_a(k, ra, i):
+        pend(xa[k].at[ra, lo], a_s.at[k], a_r.at[k, ra, i]).wait_recv()
 
     @jax.named_scope("gather")
     def gather_all(h, ra, go):
@@ -179,23 +180,31 @@
             if go:
                 send_b(k, h, ra)
 
+    pl.loop(0, early // 2)(jax.named_scope("shared")(shared))
+    if ring4:
+        seq = [0, 3, 1, 2]
+        for k in order:
+            wait_a(k, 3, 0)
+            send(xa[k].at[3, lo], xa[k].at[2, lo], a_s.at[k], a_r.at[k, 2, 0], k, 1)
+            wait_a(k, 1, 0)
+            send(xa[k].at[1, hi], xa[k].at[2, hi], a_s.at[k], a_r.at[k, 2, 1], k, 3)
+    else:
+        seq = list(range(R))
+        for r in near:
+            for k in order:
+                wait_a(k, r, 0)
+    for k in order:
+        send_b(k, 0, 0)
+    pl.loop(early // 2, early)(jax.named_scope("shared")(shared))
     for k in order:
         with jax.named_scope("wait_m"):
             pend(meta.at[k, 1:R], m_s.at[k], m_r.at[k]).wait_recv()
-    if ring4:
-        for k in order:
-            wait_a(k, 3)
-            send(xa[k].at[3, lo], xa[k].at[2, lo], a_s.at[k], a_r.at[k, 2], k, 1)
-            wait_a(k, 1)
-            send(xa[k].at[1, hi], xa[k].at[2, hi], a_s.at[k], a_r.at[k, 2], k, 3)
-        seq = [0, 3, 1, 2]
-
-        @pl.loop(0, 2)
-        def _(i):
-            gather_all(0, 3 - 2 * i, True)
-    else:
-        seq = list(range(R))
-    pl.loop(early, n_sh - R)(jax.named_scope("shared")(shared))
+    for ra in seq[1:]:
+        for k in order:
+            if ring4 and ra == 2:
+                wait_a(k, ra, 0)
+            wait_a(k, ra, 1)
+        gather_all(0, ra, True)
 
     w_copies = [
         pltpu.make_async_copy(src, dst, w_sem.at[i])
@@ -204,25 +213,23 @@
     for c in w_copies:
         c.start()
 
-    for ra in [2] if ring4 else seq[1:]:
-        for k in order:
-            wait_a(k, ra)
-        gather_all(0, ra, True)
-
     @pl.loop(0, R)
     def _(ra):
         gather_all(1, ra, False)
 
-    @pl.loop(0, R)
+    @pl.loop(0, late)
     def _(i):
-        with jax.named_scope("shared"):
-            shared(n_sh - R + i)
         for step, ra in enumerate(seq):
-            @pl.when(i == step)
+            @pl.when(i == 2 * step)
             def _():
                 relay_c(0, ra)
                 for k in order:
                     send_b(k, 1, ra)
+
+        @pl.when(early + i < n_sh)
+        @jax.named_scope("shared")
+        def _():
+            shared(early + i)
 
     for c in w_copies:
         c.wait()
@@ -319,7 +326,7 @@
         def _():
             own_b2(h)
 
-        @pl.when(t == R)
+        @pl.when(t == R + R // 2 - 1)
         def _():
             relay_b2(0)
 
@@ -467,7 +474,7 @@
             + [pltpu.VMEM((R * R * S, D), BF16), pltpu.VMEM((R * R * S, FF), BF16), pltpu.VMEM((T, D), F32)]
             + [pltpu.VMEM((2, D, tile), BF16), pltpu.VMEM((2, D, tile), BF16), pltpu.VMEM((2, tile, D), BF16)]
             + [dma((3,)), dma((4,)), dma((3,)), dma((2, 3))]
-            + [dma((3,))] * 3 + [dma((3, R))]
+            + [dma((3,))] * 3 + [dma((3, R, 2))]
             + [dma((3, HALVES)), dma((3, HALVES, R)), dma((3, HALVES)), dma((3, HALVES))]
             + [dma((3, HALVES)), dma((3, HALVES, R)), dma((3, HALVES)), dma((3, HALVES))] + [dma((3,))] * 2 + [dma((3, 2))]
             + [pltpu.SemaphoreType.REGULAR((3, HALVES))] * 2

time: 163 us -> 163 us (level)
  no operation moved by 1% of the time
where the time goes in v7:
time: 163 us
  Pallas kernels  163 us (100%)
    pallas_call x1, Pallas kernels, step(): pl.pallas_call(functools.partial(kernel, R, parts, tile, top, slots, name...  161 us

profile of v7, /device:TPU:0, one launch (start us, length us, event | category | flops | bytes accessed | tf_op | source)
XLA Modules:
  0.0 163.1 jit_solution(10765075894076632306)
XLA Ops:
  0.0 160.8 %moe.1.src = bf16[256,2048]{1,0:T(8,128)(2,1)} custom-call(bf16[256,2048]{1,0:T(8,128)(2,1)} %bitcast.17, s32[6,1,256]{2,1,0:T(1,128)} %bitcast.18, s32[6,1,256]{2,1,0:T(1,128)} %bitcast.19, f32[6,1,256]{2,1,0:T(1,128)} %bitcast.20, bf16[2048,1408]{1,0:T(8,128)(2,1)} %bitcast.14, bf16[2048,1408]{1,0:T(8,128)(2,1)} %bitcast.15, bf16[1408,2048]{1,0:T(8,128)(2,1)} %bitcast.16, ...), custom_call_target="tpu_custom_call" | custom-call | tf_op jit(solution)/shard_map/moe/pallas_call | solution.py:482
  160.8 2.1 %hand_on.1 = bf16[256,2048]{1,0:T(8,128)(2,1)} custom-call(bf16[256,2048]{1,0:T(8,128)(2,1)} %moe.1.src), custom_call_target="tpu_custom_call" | custom-call | tf_op jit(solution)/shard_map/hand_on/pallas_call | solution.py:494

commit v8 on v7

--- a/solution.py
+++ b/solution.py
@@ -269,7 +269,7 @@
 
     @jax.named_scope("relay_b2")
     def relay_b2(h):
-        for ce in range(R - 1, 0, -1):
+        for ce in range(1, R):
             for k in order:
                 pend(g_buf[k].at[h, 1], c2_s.at[k, h], c2_r.at[k, h, ce]).wait_recv()
                 for rb in near:
@@ -280,9 +280,10 @@
 
     @pl.loop(0, HALVES * R)
     def _(t):
-        h, rx = t // R, lax.rem(t, R)
-
-        @pl.when(rx == 0)
+        h, i = t // R, lax.rem(t, R)
+        rx = R - 1 - i
+
+        @pl.when(i == 0)
         @jax.named_scope("wait_c")
         def _():
             for k in range(3):
@@ -311,7 +312,7 @@
                 o = jnp.dot(hb[...], wd[:, cols[k]], preferred_element_type=F32)
                 z_buf[k][h, rx] = o.astype(BF16).reshape(R, R, S, parts[k])
 
-        @pl.when(rx == 0)
+        @pl.when(i == 0)
         def _():
             for k in range(3):
                 pl.semaphore_wait(h_free.at[k, h], R - 1)
@@ -322,11 +323,11 @@
         def _():
             relay_c(1, seq[-1])
 
-        @pl.when(rx == R - 1)
+        @pl.when(i == R - 1)
         def _():
             own_b2(h)
 
-        @pl.when(t == R + R // 2 - 1)
+        @pl.when(t == R)
         def _():
             relay_b2(0)
 

time: 163 us -> 163 us (level)
  no operation moved by 1% of the time
where the time goes in v8:
time: 163 us
  Pallas kernels  163 us (100%)
    pallas_call x1, Pallas kernels, step(): pl.pallas_call(functools.partial(kernel, R, parts, tile, top, slots, name...  161 us

profile of v8, /device:TPU:0, one launch (start us, length us, event | category | flops | bytes accessed | tf_op | source)
XLA Modules:
  0.0 162.9 jit_solution(2378085652202614371)
XLA Ops:
  0.0 160.6 %moe.1.src = bf16[256,2048]{1,0:T(8,128)(2,1)} custom-call(bf16[256,2048]{1,0:T(8,128)(2,1)} %bitcast.17, s32[6,1,256]{2,1,0:T(1,128)} %bitcast.18, s32[6,1,256]{2,1,0:T(1,128)} %bitcast.19, f32[6,1,256]{2,1,0:T(1,128)} %bitcast.20, bf16[2048,1408]{1,0:T(8,128)(2,1)} %bitcast.14, bf16[2048,1408]{1,0:T(8,128)(2,1)} %bitcast.15, bf16[1408,2048]{1,0:T(8,128)(2,1)} %bitcast.16, ...), custom_call_target="tpu_custom_call" | custom-call | tf_op jit(solution)/shard_map/moe/pallas_call | solution.py:483
  160.6 2.1 %hand_on.1 = bf16[256,2048]{1,0:T(8,128)(2,1)} custom-call(bf16[256,2048]{1,0:T(8,128)(2,1)} %moe.1.src), custom_call_target="tpu_custom_call" | custom-call | tf_op jit(solution)/shard_map/hand_on/pallas_call | solution.py:495

commit v9 on v8

--- a/solution.py
+++ b/solution.py
@@ -39,7 +39,7 @@
     order = sorted(range(3), key=lambda k: -parts[k])
     near = sorted(range(1, R), key=lambda r: (min(r, R - r), -r))
     ring4 = R == 4
-    back = (0, 2, 1)
+    back = (0, 1, 2)
     lo, hi = pl.ds(0, T // 2), pl.ds(T // 2, T // 2)
 
     def peer(axis, r):

time: 163 us -> 163 us (level)
  no operation moved by 1% of the time
where the time goes in v9:
time: 163 us
  Pallas kernels  163 us (100%)
    pallas_call x1, Pallas kernels, step(): pl.pallas_call(functools.partial(kernel, R, parts, tile, top, slots, name...  161 us

profile of v9, /device:TPU:0, one launch (start us, length us, event | category | flops | bytes accessed | tf_op | source)
XLA Modules:
  0.0 163.1 jit_solution(7707405576583377064)
XLA Ops:
  0.0 160.9 %moe.1.src = bf16[256,2048]{1,0:T(8,128)(2,1)} custom-call(bf16[256,2048]{1,0:T(8,128)(2,1)} %bitcast.17, s32[6,1,256]{2,1,0:T(1,128)} %bitcast.18, s32[6,1,256]{2,1,0:T(1,128)} %bitcast.19, f32[6,1,256]{2,1,0:T(1,128)} %bitcast.20, bf16[2048,1408]{1,0:T(8,128)(2,1)} %bitcast.14, bf16[2048,1408]{1,0:T(8,128)(2,1)} %bitcast.15, bf16[1408,2048]{1,0:T(8,128)(2,1)} %bitcast.16, ...), custom_call_target="tpu_custom_call" | custom-call | tf_op jit(solution)/shard_map/moe/pallas_call | solution.py:483
  160.9 2.1 %hand_on.1 = bf16[256,2048]{1,0:T(8,128)(2,1)} custom-call(bf16[256,2048]{1,0:T(8,128)(2,1)} %moe.1.src), custom_call_target="tpu_custom_call" | custom-call | tf_op jit(solution)/shard_map/hand_on/pallas_call | solution.py:495
